TPU v7x, 8 devices: a whole 2x2x1 slice. The times are simulated.
8 devices in a mesh: batch: 2 (over z, y), t: 4 (over x, core).
Axes of the slice: x: 2, y: 2, z: 1, core: 2. Of those that a mesh axis runs over, the one named last changes fastest.
Arguments:
- z: bfloat16 [16, 32, 64, 256], P(('batch', 't')), parts along dimension 0
- w: bfloat16 [5, 3, 3, 3, 256, 256], replicated
- b: float32 [5, 256], replicated
- gamma: float32 [4, 256], replicated
- beta: float32 [4, 256], replicated
Outputs:
- output: bfloat16 [32, 64, 128, 256], P(('batch', 't')), parts along dimension 0
There are 2 independent parts. A program takes and returns all parts, laid end to end along the dimension named above; an argument that names none is the same for every part.
All inputs are finite; a program needn't handle non-finite values.
Results may differ from a plain program's by a relative error of at most 0.0150017.
Values are sent between devices in bfloat16 or wider.
A program may use at most 1 GiB of HBM per device.

v0:
```python
import jax
import jax.numpy as jnp
from jax import lax
from jax.sharding import PartitionSpec as P

GROUPS = 32
EPS = 1e-6
DN = ('NDHWC', 'DHWIO', 'NDHWC')


def solution(mesh):
    nt = mesh.shape['t']
    perm = [(i, i + 1) for i in range(nt - 1)]

    def from_prev(x, k, r):
        got = lax.ppermute(x[-k:], 't', perm)
        return jnp.where(r == 0, jnp.broadcast_to(x[:1], got.shape), got)

    def conv_full(xp, wk, bk):
        y = lax.conv_general_dilated(xp[None], wk, (1, 1, 1), ((0, 0), (1, 1), (1, 1)), dimension_numbers=DN, preferred_element_type=jnp.float32)[0]
        return (y + bk).astype(jnp.bfloat16)

    def conv(x, r, wk, bk):
        return conv_full(jnp.concatenate([from_prev(x, 2, r), x], axis=0), wk, bk)

    def gn_act(x, fw, cnt, g, be):
        n, hh, ww, c = x.shape
        xf = x.astype(jnp.float32).reshape(n, hh, ww, GROUPS, c // GROUPS)
        s1 = jnp.sum(jnp.sum(xf, axis=(1, 2, 4)) * fw[:, None], axis=0)
        s2 = jnp.sum(jnp.sum(xf * xf, axis=(1, 2, 4)) * fw[:, None], axis=0)
        s = lax.psum(jnp.stack([s1, s2]), 't')
        mean = s[0] / cnt
        inv = lax.rsqrt(s[1] / cnt - mean * mean + EPS)
        xn = ((xf - mean[:, None]) * inv[:, None]).reshape(x.shape) * g + be
        return jax.nn.silu(xn.astype(jnp.bfloat16).astype(jnp.float32)).astype(jnp.bfloat16)

    def block(x, r, fw, cnt, w, b, gamma, beta, i, j):
        h = conv(gn_act(x, fw, cnt, gamma[i], beta[i]), r, w[j], b[j])
        h = conv(gn_act(h, fw, cnt, gamma[i + 1], beta[i + 1]), r, w[j + 1], b[j + 1])
        return (x.astype(jnp.float32) + h.astype(jnp.float32)).astype(jnp.bfloat16)

    def local(z, w, b, gamma, beta):
        r = lax.axis_index('t')
        n, hh, ww, c = z.shape
        cnt1 = nt * n * hh * ww * (c // GROUPS)
        x = block(z, r, jnp.ones((n,), jnp.float32), cnt1, w, b, gamma, beta, 0, 0)
        hx = jnp.concatenate([from_prev(x, 1, r), x], axis=0)
        up = jnp.repeat(jnp.repeat(jnp.repeat(hx, 2, axis=0), 2, axis=1), 2, axis=2)
        u = conv_full(up, w[2], b[2])
        fw2 = jnp.ones((2 * n,), jnp.float32).at[0].set(jnp.where(r == 0, 0.0, 1.0))
        cnt2 = (nt * 2 * n - 1) * 4 * hh * ww * (c // GROUPS)
        return block(u, r, fw2, cnt2, w, b, gamma, beta, 2, 3)

    spec = P(('batch', 't'))
    return jax.shard_map(local, mesh=mesh, in_specs=(spec, P(), P(), P(), P()), out_specs=spec, check_vma=False)
```

profile of v0, /device:TPU:6, one launch (start us, length us, event | category | flops | bytes accessed | tf_op | source)
XLA Modules:
  0.0 1183.9 jit_solution(11354988600297822374)
XLA Ops:
  19.2 23.9 %collective-permute-done = bf16[2,32,64,256]{3,1,2,0:T(8,128)(2,1)} collective-permute-done((bf16[2,32,64,256]{3,1,2,0:T(8,128)(2,1)S(1)}, bf16[2,32,64,256]{3,1,2,0:T(8,128)(2,1)}, u32[]{:S(2)}, u32[]{:S(2)}) %collective-permute-start) | collective-permute-done | bytes 2097184 | tf_op jit(solution)/shard_map/ppermute | solution.py:16
  48.9 22.0 %fusion.74 = (f32[256]{0:T(256)S(1)}, f32[256]{0:T(256)S(1)}, f32[2,32,8,9,256]{4,2,3,1,0:T(8,128)}) fusion(pred[8,9]{0,1:T(8,128)(4,1)S(1)} %copy-done.15, f32[256]{0:T(256)S(1)} %bitcast.238, bf16[5,3,3,3,256,256]{5,4,3,2,1,0:T(8,128)(2,1)} %param.8, bf16[4,32,1,7,2,256]{5,3,4,1,0,2:T(8,128)(2,1)S(1)} %slice.156, bf16[4,32,1,8,9,256]{5,3,4,1,0,2:T(8,128)(2,1)S(1)} %copy.25), kind=kOutput, calls=%fused_computation.98 | convolution fusion | flops 15995633664 | bytes 13896776 | tf_op jit(solution)/shard_map/conv_general_dilated | solution.py:20
  84.9 25.3 %collective-permute-done.1 = bf16[2,32,64,256]{3,1,2,0:T(8,128)(2,1)S(1)} collective-permute-done((bf16[2,32,64,256]{3,1,2,0:T(8,128)(2,1)S(1)}, bf16[2,32,64,256]{3,1,2,0:T(8,128)(2,1)S(1)}, u32[]{:S(2)}, u32[]{:S(2)}) %collective-permute-start.1) | collective-permute-done | bytes 2097184 | tf_op jit(solution)/shard_map/ppermute | solution.py:16
  114.4 21.4 %fusion.107 = f32[2,32,8,9,256]{4,2,3,1,0:T(8,128)S(1)} fusion(bf16[5,3,3,3,256,256]{5,4,3,2,1,0:T(8,128)(2,1)} %param.8, bf16[4,32,1,7,2,256]{5,3,4,1,0,2:T(8,128)(2,1)S(1)} %slice.159, bf16[4,32,1,8,9,256]{5,3,4,1,0,2:T(8,128)(2,1)S(1)} %copy.28, pred[8,9]{0,1:T(8,128)(4,1)S(1)} %copy-done.15), kind=kOutput, calls=%fused_computation.140 | convolution fusion | flops 15986196480 | bytes 13893704 | tf_op jit(solution)/shard_map/conv_general_dilated | solution.py:20
  168.6 19.0 %reshape.187 = bf16[6,64,64,256]{3,1,2,0:T(8,128)(2,1)} reshape(bf16[6,32,2,64,256]{4,2,1,3,0:T(2,128)(2,1)} %broadcast_in_dim.60) | data formatting | bytes 25165824 | tf_op jit(solution)/shard_map/reshape | solution.py:48
  187.6 15.3 %broadcast_in_dim.61 = bf16[6,64,64,2,256]{4,1,3,2,0:T(8,128)(2,1)} broadcast(bf16[6,64,64,256]{3,1,2,0:T(8,128)(2,1)} %reshape.187), dimensions={0,1,2,4} | broadcast | bytes 37748736 | tf_op jit(solution)/shard_map/broadcast_in_dim | solution.py:48
  202.9 12.5 %pad.7 = bf16[6,64,1,136,256]{4,1,3,0,2:T(8,128)(2,1)S(1)} pad(bf16[6,64,1,128,256]{4,1,3,0,2:T(8,128)(2,1)} %bitcast.225, bf16[]{:T(256)} %constant.59), padding=0_0x0_0x0_0x1_7x0_0 | pad | bytes 51904512 | tf_op jit(solution)/shard_map/broadcast_in_dim;reshape | solution.py:20
  215.4 32.4 %copy.31 = bf16[6,64,1,8,17,256]{5,3,4,1,0,2:T(8,128)(2,1)} copy(bf16[6,64,1,8,17,256]{5,1,4,3,0,2:T(8,128)(2,1)S(1)} %bitcast.223) | data formatting | bytes 53477376 | tf_op jit(solution)/shard_map/conv_general_dilated | solution.py:20
  250.5 143.8 %fusion.3 = (f32[4,256]{1,0:T(4,128)S(1)}, f32[4,256]{1,0:T(4,128)S(1)}, f32[4,64,8,17,256]{4,2,3,1,0:T(8,128)}) fusion(pred[8,17]{0,1:T(8,128)(4,1)S(1)} %copy-done.14, f32[256]{0:T(256)S(1)} %bitcast.231, bf16[6,64,1,7,2,256]{5,3,4,1,0,2:T(8,128)(2,1)S(1)} %slice.163, bf16[6,64,1,8,17,256]{5,3,4,1,0,2:T(8,128)(2,1)} %copy.31, ...), kind=kOutput, calls=%fused_computation.14 | convolution fusion | flops 122098286592 | bytes 68691080 | tf_op jit(solution)/shard_map/conv_general_dilated | solution.py:20
  400.8 32.2 %copy.32 = f32[4,64,8,17,256]{4,1,3,2,0:T(8,128)} copy(f32[4,64,8,17,256]{4,2,3,1,0:T(8,128)} %get-tuple-element.43) | data formatting | bytes 71303168 | tf_op jit(solution)/shard_map/conv_general_dilated | solution.py:20
  433.4 22.2 %fusion.17 = bf16[4,64,128,256]{3,1,2,0:T(8,128)(2,1)} fusion(f32[256]{0:T(256)S(1)} %bitcast.243, f32[256]{0:T(256)S(1)} %bitcast.242, f32[256]{0:T(256)S(1)} %mul.205, f32[256]{0:T(256)S(1)} %sub.91, f32[256]{0:T(256)S(1)} %bitcast.232, f32[4,64,1,136,256]{4,1,3,0,2:T(8,128)} %bitcast.214), kind=kLoop, calls=%fused_computation.30 | loop fusion | flops 117440512 | bytes 50336768 | tf_op jit(solution)/shard_map/convert_element_type | solution.py:35
  473.0 85.7 %collective-permute-done.3 = bf16[2,64,128,256]{3,1,2,0:T(8,128)(2,1)S(1)} collective-permute-done((bf16[2,64,128,256]{3,1,2,0:T(8,128)(2,1)}, bf16[2,64,128,256]{3,1,2,0:T(8,128)(2,1)S(1)}, u32[]{:S(2)}, u32[]{:S(2)}) %collective-permute-start.3) | collective-permute-done | bytes 8388640 | tf_op jit(solution)/shard_map/ppermute | solution.py:16
  569.8 12.5 %pad.9 = bf16[6,64,1,136,256]{4,1,3,0,2:T(8,128)(2,1)S(1)} pad(bf16[6,64,1,128,256]{4,1,3,0,2:T(8,128)(2,1)} %maximum_bitcast_fusion, bf16[]{:T(256)} %constant.59), padding=0_0x0_0x0_0x1_7x0_0 | pad | bytes 51904512 | tf_op jit(solution)/shard_map/broadcast_in_dim | solution.py:20
  582.3 32.4 %copy.34 = bf16[6,64,1,8,17,256]{5,3,4,1,0,2:T(8,128)(2,1)} copy(bf16[6,64,1,8,17,256]{5,1,4,3,0,2:T(8,128)(2,1)S(1)} %bitcast.224) | data formatting | bytes 53477376 | tf_op jit(solution)/shard_map/conv_general_dilated | solution.py:20
  617.4 144.2 %fusion.6 = (f32[4,256]{1,0:T(4,128)S(1)}, f32[4,256]{1,0:T(4,128)S(1)}, f32[4,64,8,17,256]{4,2,3,1,0:T(8,128)}) fusion(pred[8,17]{0,1:T(8,128)(4,1)S(1)} %copy-done.14, f32[256]{0:T(256)S(1)} %bitcast.235, bf16[6,64,1,7,2,256]{5,3,4,1,0,2:T(8,128)(2,1)S(1)} %slice.167, bf16[6,64,1,8,17,256]{5,3,4,1,0,2:T(8,128)(2,1)} %copy.34, ...), kind=kOutput, calls=%fused_computation.17 | convolution fusion | flops 122098286592 | bytes 68691080 | tf_op jit(solution)/shard_map/conv_general_dilated | solution.py:20
  768.3 20.8 %copy.35 = f32[4,64,8,17,256]{4,1,3,2,0:T(8,128)S(1)} copy(f32[4,64,8,17,256]{4,2,3,1,0:T(8,128)} %get-tuple-element.44) | data formatting | bytes 71303168 | tf_op jit(solution)/shard_map/conv_general_dilated | solution.py:20
  789.1 13.5 %fusion.21 = bf16[4,64,128,256]{3,1,2,0:T(8,128)(2,1)} fusion(f32[4,64,1,136,256]{4,1,3,0,2:T(8,128)S(1)} %bitcast.216, f32[256]{0:T(256)S(1)} %bitcast.241, f32[256]{0:T(256)S(1)} %bitcast.240, f32[256]{0:T(256)S(1)} %mul.217, f32[256]{0:T(256)S(1)} %sub.96, f32[256]{0:T(256)S(1)} %bitcast.236), kind=kLoop, calls=%fused_computation.34 | loop fusion | flops 117440512 | bytes 50336768 | tf_op jit(solution)/shard_map/convert_element_type | solution.py:35
  819.9 85.8 %collective-permute-done.4 = bf16[2,64,128,256]{3,1,2,0:T(8,128)(2,1)S(1)} collective-permute-done((bf16[2,64,128,256]{3,1,2,0:T(8,128)(2,1)}, bf16[2,64,128,256]{3,1,2,0:T(8,128)(2,1)S(1)}, u32[]{:S(2)}, u32[]{:S(2)}) %collective-permute-start.4) | collective-permute-done | bytes 8388640 | tf_op jit(solution)/shard_map/ppermute | solution.py:16
  916.8 12.5 %pad.11 = bf16[6,64,1,136,256]{4,1,3,0,2:T(8,128)(2,1)S(1)} pad(bf16[6,64,1,128,256]{4,1,3,0,2:T(8,128)(2,1)} %maximum_bitcast_fusion.1, bf16[]{:T(256)} %constant.59), padding=0_0x0_0x0_0x1_7x0_0 | pad | bytes 51904512 | tf_op jit(solution)/shard_map/broadcast_in_dim | solution.py:20
  929.3 32.4 %copy.37 = bf16[6,64,1,8,17,256]{5,3,4,1,0,2:T(8,128)(2,1)} copy(bf16[6,64,1,8,17,256]{5,1,4,3,0,2:T(8,128)(2,1)S(1)} %bitcast.222) | data formatting | bytes 53477376 | tf_op jit(solution)/shard_map/conv_general_dilated | solution.py:20
  964.4 141.1 %broadcast_select_fusion = f32[4,64,8,17,256]{4,2,3,1,0:T(8,128)} fusion(pred[8,17]{0,1:T(8,128)(4,1)S(1)} %copy-done.14, bf16[6,64,1,7,2,256]{5,3,4,1,0,2:T(8,128)(2,1)S(1)} %slice.171, bf16[6,64,1,8,17,256]{5,3,4,1,0,2:T(8,128)(2,1)} %copy.37, bf16[3,3,3,256,256]{4,3,2,1,0:T(8,128)(2,1)S(1)} %copy-done.3), kind=kOutput, calls=%fused_computation.65 | convolution fusion | flops 122026983424 | bytes 68681864 | tf_op jit(solution)/shard_map/conv_general_dilated | solution.py:20
  1105.5 32.3 %copy.38 = f32[4,64,8,17,256]{4,1,3,2,0:T(8,128)} copy(f32[4,64,8,17,256]{4,2,3,1,0:T(8,128)} %broadcast_select_fusion) | data formatting | bytes 71303168 | tf_op jit(solution)/shard_map/conv_general_dilated | solution.py:20
  1137.8 27.9 %fusion.13 = bf16[4,64,128,256]{3,1,2,0:T(8,128)(2,1)} fusion(f32[4,64,1,136,256]{4,1,3,0,2:T(8,128)} %bitcast.217, f32[256]{0:T(256)S(1)} %bitcast.234, f32[256]{0:T(256)S(1)} %bitcast.233, f32[4,64,1,136,256]{4,1,3,0,2:T(8,128)} %bitcast.215), kind=kLoop, calls=%fused_computation.26 | loop fusion | flops 67108864 | bytes 83888128 | tf_op jit(solution)/shard_map/convert_element_type | solution.py:40
  1165.7 17.9 %copy.39 = bf16[4,64,128,256]{3,2,1,0:T(8,128)(2,1)} copy(bf16[4,64,128,256]{3,1,2,0:T(8,128)(2,1)} %fusion.13) | data formatting | bytes 33554432 | tf_op jit(solution)/shard_map/convert_element_type | solution.py:40
  (147 shorter events, 154.0 us)
Async XLA Ops:
  15.8 27.4 %collective-permute-start = (bf16[2,32,64,256]{3,1,2,0:T(8,128)(2,1)S(1)}, bf16[2,32,64,256]{3,1,2,0:T(8,128)(2,1)}, u32[]{:S(2)}, u32[]{:S(2)}) collective-permute-start(bf16[2,32,64,256]{3,1,2,0:T(8,128)(2,1)S(1)} %fusion.80), channel_id=1, source_target_pairs={{0,1},{1,2},{2,3},{4,5},{5,6},{6,7}} | collective-permute-start | bytes 6291464 | tf_op jit(solution)/shard_map/ppermute | solution.py:16
  82.9 27.4 %collective-permute-start.1 = (bf16[2,32,64,256]{3,1,2,0:T(8,128)(2,1)S(1)}, bf16[2,32,64,256]{3,1,2,0:T(8,128)(2,1)S(1)}, u32[]{:S(2)}, u32[]{:S(2)}) collective-permute-start(bf16[2,32,64,256]{3,1,2,0:T(8,128)(2,1)S(1)} %fusion.84), channel_id=1, source_target_pairs={{0,1},{1,2},{2,3},{4,5},{5,6},{6,7}} | collective-permute-start | bytes 6291464 | tf_op jit(solution)/shard_map/ppermute | solution.py:16
  140.2 16.1 %collective-permute-start.2 = (bf16[1,32,64,256]{3,1,2,0:T(8,128)(2,1)}, bf16[1,32,64,256]{3,1,2,0:T(8,128)(2,1)S(1)}, u32[]{:S(2)}, u32[]{:S(2)}) collective-permute-start(bf16[1,32,64,256]{3,1,2,0:T(8,128)(2,1)} %slice.162), channel_id=1, source_target_pairs={{0,1},{1,2},{2,3},{4,5},{5,6},{6,7}} | collective-permute-start | bytes 3145736 | tf_op jit(solution)/shard_map/ppermute | solution.py:16
  215.4 35.1 %copy-start.1 = (bf16[3,3,3,256,256]{4,3,2,1,0:T(8,128)(2,1)S(1)}, bf16[3,3,3,256,256]{4,3,2,1,0:T(8,128)(2,1)}, u32[]{:S(2)}) copy-start(bf16[3,3,3,256,256]{4,3,2,1,0:T(8,128)(2,1)} %fusion.97.clone.5) | copy-start | bytes 10616836
  215.4 35.1 %copy-start.4 = (f32[1,256]{1,0:T(1,128)S(1)}, f32[1,256]{1,0:T(1,128)}, u32[]{:S(2)}) copy-start(f32[1,256]{1,0:T(1,128)} %get-tuple-element.30) | copy-start | bytes 3076
  215.4 35.1 %copy-start.14 = (pred[8,17]{0,1:T(8,128)(4,1)S(1)}, pred[8,17]{0,1:T(8,128)(4,1)}, u32[]{:S(2)}) copy-start(pred[8,17]{0,1:T(8,128)(4,1)} %constant.85) | copy-start | bytes 412
  250.5 144.2 %copy-start.12 = (f32[4]{0:T(128)S(1)}, f32[4]{0:T(128)}, u32[]{:S(2)}) copy-start(f32[4]{0:T(128)} %scatter.4) | copy-start | bytes 52
  400.8 32.6 %copy-start.10 = (f32[1,256]{1,0:T(1,128)S(1)}, f32[1,256]{1,0:T(1,128)}, u32[]{:S(2)}) copy-start(f32[1,256]{1,0:T(1,128)} %get-tuple-element.37) | copy-start | bytes 3076
  400.8 32.6 %copy-start.11 = (f32[1,256]{1,0:T(1,128)S(1)}, f32[1,256]{1,0:T(1,128)}, u32[]{:S(2)}) copy-start(f32[1,256]{1,0:T(1,128)} %get-tuple-element.41) | copy-start | bytes 3076
  463.9 94.8 %collective-permute-start.3 = (bf16[2,64,128,256]{3,1,2,0:T(8,128)(2,1)}, bf16[2,64,128,256]{3,1,2,0:T(8,128)(2,1)S(1)}, u32[]{:S(2)}, u32[]{:S(2)}) collective-permute-start(bf16[2,64,128,256]{3,1,2,0:T(8,128)(2,1)} %slice.166), channel_id=1, source_target_pairs={{0,1},{1,2},{2,3},{4,5},{5,6},{6,7}} | collective-permute-start | bytes 25165832 | tf_op jit(solution)/shard_map/ppermute | solution.py:16
  465.8 93.8 %slice-start.4 = ((s8[16777216]{0:T(1024)(128)(4,1)}), s8[4194304]{0:T(1024)(128)(4,1)S(1)}, s32[]{:S(2)}) async-start(s8[16777216]{0:T(1024)(128)(4,1)} %bitcast.220), calls=%async_computation.4 | async-start | bytes 8388608
  470.3 89.3 %slice-start.5 = ((s8[16777216]{0:T(1024)(128)(4,1)}), s8[4194304]{0:T(1024)(128)(4,1)S(1)}, s32[]{:S(2)}) async-start(s8[16777216]{0:T(1024)(128)(4,1)} %bitcast.220), calls=%async_computation.5 | async-start | bytes 8388608
  472.9 86.7 %slice-start.6 = ((s8[16777216]{0:T(1024)(128)(4,1)}), s8[4194304]{0:T(1024)(128)(4,1)S(1)}, s32[]{:S(2)}) async-start(s8[16777216]{0:T(1024)(128)(4,1)} %bitcast.220), calls=%async_computation.6 | async-start | bytes 8388608
  472.9 86.7 %slice-start.7 = ((s8[16777216]{0:T(1024)(128)(4,1)}), s8[4194304]{0:T(1024)(128)(4,1)S(1)}, s32[]{:S(2)}) async-start(s8[16777216]{0:T(1024)(128)(4,1)} %bitcast.220), calls=%async_computation.7 | async-start | bytes 8388608
  582.3 35.1 %copy-start.2 = (bf16[3,3,3,256,256]{4,3,2,1,0:T(8,128)(2,1)S(1)}, bf16[3,3,3,256,256]{4,3,2,1,0:T(8,128)(2,1)}, u32[]{:S(2)}) copy-start(bf16[3,3,3,256,256]{4,3,2,1,0:T(8,128)(2,1)} %fusion.96.clone.5) | copy-start | bytes 10616836
  582.3 35.1 %copy-start.7 = (f32[1,256]{1,0:T(1,128)S(1)}, f32[1,256]{1,0:T(1,128)}, u32[]{:S(2)}) copy-start(f32[1,256]{1,0:T(1,128)} %get-tuple-element.33) | copy-start | bytes 3076
  617.4 144.6 %copy-start.13 = (f32[4]{0:T(128)S(1)}, f32[4]{0:T(128)}, u32[]{:S(2)}) copy-start(f32[4]{0:T(128)} %scatter.4) | copy-start | bytes 52
  811.0 94.8 %collective-permute-start.4 = (bf16[2,64,128,256]{3,1,2,0:T(8,128)(2,1)}, bf16[2,64,128,256]{3,1,2,0:T(8,128)(2,1)S(1)}, u32[]{:S(2)}, u32[]{:S(2)}) collective-permute-start(bf16[2,64,128,256]{3,1,2,0:T(8,128)(2,1)} %slice.170), channel_id=1, source_target_pairs={{0,1},{1,2},{2,3},{4,5},{5,6},{6,7}} | collective-permute-start | bytes 25165832 | tf_op jit(solution)/shard_map/ppermute | solution.py:16
  812.9 93.8 %slice-start = ((s8[16777216]{0:T(1024)(128)(4,1)}), s8[4194304]{0:T(1024)(128)(4,1)S(1)}, s32[]{:S(2)}) async-start(s8[16777216]{0:T(1024)(128)(4,1)} %bitcast.218), calls=%async_computation | async-start | bytes 8388608
  817.2 89.4 %slice-start.1 = ((s8[16777216]{0:T(1024)(128)(4,1)}), s8[4194304]{0:T(1024)(128)(4,1)S(1)}, s32[]{:S(2)}) async-start(s8[16777216]{0:T(1024)(128)(4,1)} %bitcast.218), calls=%async_computation.1 | async-start | bytes 8388608
  819.9 86.7 %slice-start.2 = ((s8[16777216]{0:T(1024)(128)(4,1)}), s8[4194304]{0:T(1024)(128)(4,1)S(1)}, s32[]{:S(2)}) async-start(s8[16777216]{0:T(1024)(128)(4,1)} %bitcast.218), calls=%async_computation.2 | async-start | bytes 8388608
  819.9 86.7 %slice-start.3 = ((s8[16777216]{0:T(1024)(128)(4,1)}), s8[4194304]{0:T(1024)(128)(4,1)S(1)}, s32[]{:S(2)}) async-start(s8[16777216]{0:T(1024)(128)(4,1)} %bitcast.218), calls=%async_computation.3 | async-start | bytes 8388608
  929.3 35.1 %copy-start.3 = (bf16[3,3,3,256,256]{4,3,2,1,0:T(8,128)(2,1)S(1)}, bf16[3,3,3,256,256]{4,3,2,1,0:T(8,128)(2,1)}, u32[]{:S(2)}) copy-start(bf16[3,3,3,256,256]{4,3,2,1,0:T(8,128)(2,1)} %fusion.151) | copy-start | bytes 10616836
  1105.5 32.3 %copy-start.6 = (f32[1,256]{1,0:T(1,128)S(1)}, f32[1,256]{1,0:T(1,128)}, u32[]{:S(2)}) copy-start(f32[1,256]{1,0:T(1,128)} %get-tuple-element.29) | copy-start | bytes 3076
  (5 other events, 79.1 us)
where the time goes:
time: 1190 us; the launch traced here: 1180 us
  matrix products  473 us (40%)
  local copies, waits for them, and re-layouts  347 us (29%)
  waiting for transfers between devices  230 us (19%)
  other arithmetic  99.3 us (8%)
  blocking collectives  23.7 us (2%)
    conv_general_dilated x5, matrix products, conv_full(): lax.conv_general_dilated(xp[None], wk, (1, 1, 1), ((0, 0), (1, 1), (1, 1)...  473 us
    ppermute x5, waiting for transfers between devices, from_prev(): got = lax.ppermute(x[-k:], 't', perm)  230 us
    conv_general_dilated x16, local copies, waits for them, and re-layouts, conv_full(): lax.conv_general_dilated(xp[None], wk, (1, 1, 1), ((0, 0), (1, 1), (1, 1)...  206 us
    convert_element_type x4, other arithmetic, gn_act(): jax.nn.silu(xn.astype(jnp.bfloat16).astype(jnp.float32))  40.6 us
    convert_element_type x2, other arithmetic, block(): return (x.astype(jnp.float32) + h.astype(jnp.float32)).astype(jnp.bfloat16)  29.6 us
    broadcast_in_dim x3, local copies, waits for them, and re-layouts, local(): up = jnp.repeat(jnp.repeat(jnp.repeat(hx, 2, axis=0), 2, axis=1), 2, axis=2)  27.2 us
    broadcast_in_dim x4, local copies, waits for them, and re-layouts, conv_full(): xp[None]  26 us
  transfers between devices with their start and end apart: 5, of which 5 were waited for; matrix products, arithmetic and copies ran while one was open for 2% of the time, Pallas kernels for 0%

commit v1 on v0

v1 whole, which is shorter than its diff:
```python
import functools
import jax
import jax.numpy as jnp
from jax import lax
from jax.experimental import pallas as pl
from jax.experimental.pallas import tpu as pltpu
from jax.sharding import PartitionSpec as P

GROUPS = 32
EPS = 1e-6
C = 256
S = 16
LANES = 128
TAPS = 27
BF = jnp.bfloat16
F32 = jnp.float32
PAIR = (0, 1)
BOTH = [(slice(None, LANES)), (slice(LANES, None))]
MESH = pl.DeviceIdType.MESH
SMEM = pl.BlockSpec(memory_space=pltpu.SMEM)
VMEM = pl.BlockSpec(memory_space=pltpu.VMEM)
PARAMS = pltpu.CompilerParams(vmem_limit_bytes=58 * 2**20)


def sds(*shape, dtype=BF):
    return jax.ShapeDtypeStruct(shape, dtype)


def whole(*shape, lead=0):
    index = (lead,) + (0,) * (len(shape) - 1)
    return pl.BlockSpec(shape, lambda t: index, pipeline_mode=pl.Buffered(1))


def cost(flops, nbytes):
    return pl.CostEstimate(flops=flops, bytes_accessed=nbytes, transcendentals=0)


def silu(v):
    return v / (1.0 + jnp.exp(-v))


def sublane():
    return lax.broadcasted_iota(jnp.int32, (S, C), 0)


def shifted(v, down):
    edge, by = (0, 1) if down else (S - 1, S - 1)
    return jnp.where(sublane() == edge, 0.0, pltpu.roll(v, by, 0)).astype(BF)


def spread(mxu_items, vpu_items, lead):
    n, m = len(mxu_items), len(vpu_items)
    done = 0
    for k, item in enumerate(mxu_items):
        item()
        want = 0 if k < lead else -(-m * (k - lead + 1) // (n - lead))
        for go in vpu_items[done:want]:
            go()
        done = max(done, want)
    for go in vpu_items[done:]:
        go()


def add_sums(st_ref, frame, rows):
    v = rows.astype(F32).reshape(-1, 8, C)
    st_ref[frame, 0] += jnp.sum(v, axis=0)
    st_ref[frame, 1] += jnp.sum(v * v, axis=0)


def conv_body(H, J, R, wi, nf, nsub, has_res, natural, aliased, *refs):
    it = iter(refs)
    first_ref, gn_ref, b_ref = (next(it) for _ in range(3))
    frames = [next(it) for _ in range(nf)]
    w_ref = next(it)
    res_ref = next(it) if has_res else None
    if aliased:
        next(it)
    out_ref = next(it)
    st_ref = None if natural else next(it)
    xs = next(it)
    nat = next(it) if natural else None
    HR = (5 - nf) * R
    nblk = H // (2 * HR)
    last = nblk + 1
    HP = H + 2 + 4 * HR
    PT = 4
    NP = J // PT
    of = lambda q: q * (nf - 3)
    orow = lambda q, r: r + q * R * (4 - nf)

    def half_steps(t, u, accA, accB, dum):
        base = u * 2 * HR

        def act_item(f, r, j):
            def go():
                v = frames[f][0, base + r, j].astype(F32)
                if f < nsub:
                    v = jnp.where(first_ref[0] == 1, frames[nsub][0, base + r, j].astype(F32), v)
                xn = ((v - gn_ref[0:1, :]) * gn_ref[1:2, :] + gn_ref[2:3, :]).astype(BF).astype(F32)
                s = jnp.where(t < nblk, silu(xn), 0.0)
                dst = f * HP + t * (2 * HR) + r + 1
                xs[dst, j + 1] = s.astype(BF)
                if j == 0:
                    xs[dst, J + 1] = shifted(s, False)
                if j == J - 1:
                    xs[dst, 0] = shifted(s, True)
            return go

        def act_items(half):
            return [act_item(f, half * HR + r, j) for r in range(HR) for f in range(nf) for j in range(J)]

        def act_only():
            def go(r, _):
                for f in range(nf):
                    for j in range(J):
                        act_item(f, r, j)()
                return 0
            lax.fori_loop(0, jnp.where(t == 0, 2 * HR, HR), go, 0)

        def pop_item(acc, q, half, r, piece):
            def go():
                row = base + half * HR + orow(q, r)
                tiles = pl.ds(piece * PT, PT)
                v = pltpu.matmul_pop(acc) + b_ref[wi:wi + 1, :]
                ob = v.astype(BF)
                if has_res:
                    h = ob.astype(F32) + res_ref[of(q), row, tiles].astype(F32).reshape(PT * S, C)
                    ob = h.astype(BF)
                if natural:
                    for k in range(PT):
                        for part, cols in zip(PAIR, BOTH):
                            nat[r, q, part, pl.ds(piece * PT + k, S, stride=J), :] = h[k * S:(k + 1) * S, cols]
                    if piece == NP - 1:
                        for part, cols in zip(PAIR, BOTH):
                            out_ref[of(q), row, :, cols] = nat[r, q, part].astype(BF)
                else:
                    out_ref[of(q), row, tiles] = ob.reshape(PT, S, C)
                    add_sums(st_ref, of(q), ob)
            return go

        def pops(accs, half):
            return [pop_item(accs[q][r][p], q, half, r, p) for r in range(R) for q in PAIR for p in range(NP)]

        def mxu_item(accs, y0, n, r, p, half):
            kt, kh, kw = n // 9, n // 3 % 3, n % 3
            reg = (n + half) % 2
            lead = r == 0 and p == 0

            def go():
                for q in PAIR:
                    lhs = xs[(of(q) + kt) * HP + y0 + orow(q, r) + kh, pl.ds(kw + p * PT, PT)].reshape(PT * S, C)
                    pltpu.matmul_acc_lhs(accs[q][r][p], lhs, load_staged_rhs=reg if lead else None)
                if lead:
                    nxt = w_ref[0, (n + 1) % TAPS]
                    for q in PAIR:
                        pltpu.matmul_push_rhs(nxt, staging_register=1 - reg, mxu_index=q)
            return go

        def mxu_items(accs, y0, half):
            return [mxu_item(accs, y0, n, r, p, half) for n in range(TAPS) for r in range(R) for p in range(NP)]

        def dummy():
            for q in PAIR:
                pltpu.matmul_acc_lhs(dum[q], jnp.zeros((S, C), BF), load_staged_rhs=1)
                pltpu.matmul_pop(dum[q])

        @pl.when(t == 0)
        def _():
            for accs in (accA, accB):
                for q in PAIR:
                    for a in sum(accs[q], []):
                        pltpu.matmul_pop(a)
            for f in range(nf):
                xs[f * HP] = jnp.zeros((J + 2, S, C), BF)

        if not natural:
            @pl.when(t == 2)
            def _():
                st_ref[...] = jnp.zeros_like(st_ref)

        @pl.when(t < 2)
        def _():
            act_only()

        @pl.when(t >= 2)
        def _():
            spread(mxu_items(accA, (t - 2) * (2 * HR) + HR, 0), pops(accB, 0) + act_items(0), 4)

        @pl.when(t == 0)
        def _():
            dummy()
            for q in PAIR:
                pltpu.matmul_push_rhs(w_ref[0, 0], staging_register=1, mxu_index=q)

        @pl.when((t >= 1) & (t < last))
        def _():
            spread(mxu_items(accB, (t - 1) * (2 * HR), 1), pops(accA, 1) + act_items(1), 4)

        @pl.when(t == last)
        def _():
            dummy()
            for g in pops(accA, 1):
                g()

    def body(*accs):
        def step(u, _):
            half_steps(2 * pl.program_id(0) + u, u, *accs)
            return 0
        lax.fori_loop(0, 2, step, 0)

    acc = lambda q: [[pltpu.ACC(q)((PT * S, C), F32) for _ in range(NP)] for _ in range(R)]
    pl.run_scoped(body, [acc(0), acc(1)], [acc(0), acc(1)], [pltpu.ACC(q)((S, C), F32) for q in PAIR])


def conv(frames, w27, b, gn, first, wi, nsub=0, res=None, natural=False, ybuf=None):
    nf, nout = len(frames), len(frames) - 2
    _, H, J, _, _ = frames[0][0].shape
    R = 2
    rows = 4 * R * (5 - nf)
    nst = H // rows
    HP = H + 2 + rows
    outi = lambda t: jnp.maximum(t - 1, 0)
    late = pl.BlockSpec((nout, rows, J, S, C), lambda t: (0, outi(t), 0, 0, 0))
    now = lambda k: pl.BlockSpec((1, rows, J, S, C), lambda t: (k, jnp.minimum(t, nst - 1), 0, 0, 0))
    in_specs = [SMEM, whole(8, C), whole(5, C)] + [now(k) for _, k in frames] + [whole(1, TAPS, C, C, lead=wi)]
    args = [first, gn, b] + [a for a, _ in frames] + [w27]
    scratch = [pltpu.VMEM((nf * HP, J + 2, S, C), BF)]
    if res is not None:
        in_specs.append(late)
        args.append(res)
    if natural:
        fi = 1 if ybuf is None else 0
        if ybuf is not None:
            in_specs.append(pl.BlockSpec(memory_space=pl.ANY))
            args.append(ybuf)
        oshape, ospec = sds(2 * nout, H, J * S, C), pl.BlockSpec((nout, rows, J * S, C), lambda t: (fi, outi(t), 0, 0))
        scratch.append(pltpu.VMEM((R, 2, 2, J * S, LANES), F32))
    else:
        oshape, ospec = [sds(nout, H, J, S, C), sds(nout, 2, 8, C, dtype=F32)], [late, whole(nout, 2, 8, C)]
    return pl.pallas_call(
        functools.partial(conv_body, H, J, R, wi, nf, nsub, res is not None, natural, ybuf is not None),
        grid=(nst + 1,),
        in_specs=in_specs,
        out_specs=ospec,
        out_shape=oshape,
        input_output_aliases={} if ybuf is None else {len(args) - 1: 0},
        scratch_shapes=scratch,
        compiler_params=PARAMS,
        cost_estimate=cost(2 * nout * H * J * S * TAPS * C * C, 6 * nout * H * J * S * C),
        name=f"conv{wi}_{nout}{nsub}" + ("n" if natural else "t"),
    )(*args)


HU, JU, PADR, HPU, NS = 32, 4, 4, 40, 3
KINDS = [(tt, hh, ww) for tt in PAIR for hh in PAIR for ww in PAIR]
SEQ = [(n, kt, kh, kw) for n, kind in enumerate(KINDS)
       for kt in range(kind[0], 3 - kind[0], 2) for kh in range(kind[1], 3 - kind[1], 2) for kw in range(kind[2], 3 - kind[2], 2)]


def up_body(from_halo, first_ref, b_ref, xa_ref, xb_ref, w_ref, u_ref, st_ref, xs, es):
    t = pl.program_id(0)
    last = HU // 4 + 1
    slots = [lax.rem(t + k, NS) for k in range(NS)]

    def fill(f, src):
        def go(r, _):
            row = f * HPU + PADR + r
            xs[row, 1:JU + 1] = src[0, r]
            xs[row, JU + 1] = shifted(src[0, r, 0].astype(F32), False)
            xs[row, 0] = shifted(src[0, r, JU - 1].astype(F32), True)
            return 0
        lax.fori_loop(0, HU, go, 0)

    def mxu_items(accE, accF):
        def tiles_of(n):
            ww = KINDS[n][2]
            return (accF, JU, JU + 1) if ww else (accE[n // 2 % 2], JU + 1, 0)

        def push(k):
            w = w_ref[0, SEQ[k][1] * 9 + SEQ[k][2] * 3 + SEQ[k][3]]
            for q in PAIR:
                pltpu.matmul_push_rhs(w, staging_register=k % 2, mxu_index=q)

        def acc_item(k):
            n, kt, kh, kw = SEQ[k]
            tt, hh, ww = KINDS[n]
            refs, nt, _ = tiles_of(n)
            frames = PAIR if tt else (kt // 2,)

            def go():
                if k == 0:
                    push(0)
                load = k % 2
                for f in frames:
                    for i in PAIR:
                        for q in PAIR:
                            row = 4 * t - 4 + 2 * q + i + (kh // 2 if hh == 0 else 0) + PADR
                            lhs = xs[f * HPU + row, pl.ds((kw + 1) // 2, nt)].reshape(nt * S, C)
                            pltpu.matmul_acc_lhs(refs[q][tt * f * 2 + i], lhs, load_staged_rhs=load)
                        load = None
                    if f == frames[0] and k + 1 < TAPS:
                        push(k + 1)
            return go

        def pop_item(n):
            tt, hh, ww = KINDS[n]
            refs, nt, off = tiles_of(n)

            def go():
                for ai in range(tt + 1):
                    for i in PAIR:
                        for q in PAIR:
                            es[slots[0], q, tt + ai, hh, i, off:off + nt] = pltpu.matmul_pop(refs[q][2 * ai + i]).reshape(nt, S, C)
            return go

        items = []
        for k, (n, *_) in enumerate(SEQ):
            items.append(acc_item(k))
            if n and SEQ[k - 1][0] != n:
                items.append(pop_item(n - 1))
        return items + [pop_item(len(KINDS) - 1)]

    def combine_item(q, half):
        cols = BOTH[half]

        def sums(slot, qq, hh, i, w):
            e, f0, f1 = (es[slot, qq, k, hh, i, w, :, cols] for k in range(3))
            return e + f0, e + f1

        def rows_of(w):
            e = []
            for k in range(3):
                d = 2 * q + k - 1
                e.append(sums(slots[1], 1, 0, 1, w) if d < 0 else sums(slots[2], d // 2, 0, d % 2, w))
            f = [sums(slots[2], q, 1, i, w) for i in PAIR]
            return [[e[i + a][p] + f[i][p] for p in PAIR] for i in PAIR for a in PAIR]

        def go():
            bias = b_ref[2:3, cols]
            left = rows_of(0)
            tot = [[jnp.zeros((8, LANES), F32) for _ in PAIR] for _ in PAIR]
            for j in range(JU):
                mid, right = rows_of(JU + 1 + j), rows_of(j + 1)
                for o in range(4):
                    for p in PAIR:
                        m = mid[o][p] + bias
                        for bc, side in zip(PAIR, (left, right)):
                            ob = (side[o][p] + m).astype(BF)
                            u_ref[p, 4 * q + o, 2 * j + bc, :, cols] = ob
                            v = ob.astype(F32).reshape(2, 8, LANES)
                            tot[p][0] += jnp.sum(v, axis=0)
                            tot[p][1] += jnp.sum(v * v, axis=0)
                left = right
            for p in PAIR:
                for z in PAIR:
                    st_ref[p, z, :, cols] += tot[p][z]
        return go

    def body(accE, accF):
        combine = [combine_item(q, half) for q in PAIR for half in PAIR]

        @pl.when(t == 0)
        def _():
            for q in PAIR:
                for a in accE[0][q] + accE[1][q] + accF[q]:
                    pltpu.matmul_pop(a)
            for f in PAIR:
                for r in list(range(PADR)) + list(range(PADR + HU, HPU)):
                    xs[f * HPU + r] = jnp.zeros((JU + 2, S, C), BF)
            fill(1, xb_ref)
            if from_halo:
                @pl.when(first_ref[0] == 1)
                def _():
                    fill(0, xb_ref)

                @pl.when(first_ref[0] == 0)
                def _():
                    fill(0, xa_ref)
            else:
                fill(0, xa_ref)

        @pl.when(t == 2)
        def _():
            st_ref[...] = jnp.zeros_like(st_ref)

        @pl.when(t < last)
        def _():
            spread(mxu_items(accE, accF), combine, 2)

        @pl.when(t == last)
        def _():
            for g in combine:
                g()

    refs = lambda tiles: [[pltpu.ACC(q)((tiles * S, C), F32) for _ in range(4)] for q in PAIR]
    pl.run_scoped(body, [refs(JU + 1), refs(JU + 1)], refs(JU))


def up_conv(xa, xb, w27, b, first, from_halo):
    frame = (1, HU, JU, S, C)
    return pl.pallas_call(
        functools.partial(up_body, from_halo),
        grid=(HU // 4 + 2,),
        in_specs=[SMEM, whole(5, C), whole(*frame), whole(*frame), whole(1, TAPS, C, C, lead=2)],
        out_specs=[pl.BlockSpec((2, 8, 2 * JU, S, C), lambda t: (0, jnp.clip(t - 2, 0, HU // 4 - 1), 0, 0, 0)), whole(2, 2, 8, C)],
        out_shape=[sds(2, 2 * HU, 2 * JU, S, C), sds(2, 2, 8, C, dtype=F32)],
        scratch_shapes=[pltpu.VMEM((2 * HPU, JU + 2, S, C), BF), pltpu.VMEM((NS, 2, 3, 2, 2, 2 * JU + 1, S, C), F32)],
        compiler_params=PARAMS,
        cost_estimate=cost(2 * xb.size * TAPS * C, 10 * xb.size),
        name="up" + ("h" if from_halo else ""),
    )(first, b, xa, xb, w27)


def prep_body(z_ref, z0_ref, z1_ref, st_ref, tmp):
    @pl.when(pl.program_id(0) == 0)
    def _():
        st_ref[...] = jnp.zeros_like(st_ref)

    for f in PAIR:
        for r in range(z_ref.shape[1]):
            v = z_ref[f, r].astype(F32)
            add_sums(st_ref, f, v)
            for half, cols in zip(PAIR, BOTH):
                tmp[f, r, half] = v[:, cols]
        for r in range(z_ref.shape[1]):
            for j in range(JU):
                for half, cols in zip(PAIR, BOTH):
                    (z0_ref, z1_ref)[f][0, r, j, :, cols] = tmp[f, r, half, pl.ds(j, S, stride=JU), :].astype(BF)


def prep(z):
    rows, width = 8, JU * S
    return pl.pallas_call(
        prep_body,
        grid=(HU // rows,),
        in_specs=[pl.BlockSpec((2, rows, width, C), lambda t: (0, t, 0, 0))],
        out_specs=[pl.BlockSpec((1, rows, JU, S, C), lambda t: (0, t, 0, 0, 0))] * 2 + [whole(2, 2, 8, C)],
        out_shape=[sds(1, HU, JU, S, C)] * 2 + [sds(2, 2, 8, C, dtype=F32)],
        scratch_shapes=[pltpu.VMEM((2, rows, 2, width, LANES), F32)],
        compiler_params=PARAMS,
        cost_estimate=cost(8 * z.size, 4 * z.size),
        name="prep",
    )(z)


def stats_body(n, gi, cnt, drop, *refs):
    sts, (gamma_ref, beta_ref, gn_ref, mine, chip, recv, send_sem, recv_sem) = refs[:n], refs[n:]
    me = lax.axis_index("t")
    mate = me + 1 - 2 * lax.rem(me, 2)
    barrier = pltpu.get_barrier_semaphore()
    for d in range(1, 4):
        pl.semaphore_signal(barrier, inc=1, device_id={"t": lax.rem(me + d, 4)}, device_id_type=MESH)
    keep = jnp.where(me == 0, 0.0, 1.0) if drop else 1.0
    for z in PAIR:
        tot = None
        for st in sts:
            for f in range(st.shape[0]):
                v = st[f, z]
                if drop and st is sts[0] and f == 0:
                    v = v * keep
                tot = v if tot is None else tot + v
        mine[z] = tot
    pl.semaphore_wait(barrier, 3)

    def copy(src, slot, dev, sem):
        return pltpu.make_async_remote_copy(
            src_ref=src, dst_ref=recv.at[slot], send_sem=send_sem.at[sem], recv_sem=recv_sem.at[slot],
            device_id={"t": dev}, device_id_type=MESH)

    swap = copy(mine, 0, mate, 0)
    swap.start()
    swap.wait()
    chip[...] = mine[...] + recv[0]

    @pl.when(me == 0)
    def _():
        out = [copy(chip, 1, 2, 1), copy(chip, 1, 3, 2)]
        for c in out:
            c.start()
        for c in out:
            c.wait_send()

    @pl.when(me >= 2)
    def _():
        c = copy(chip, 1, me - 2, 1)
        c.start()
        c.wait_send()

    copy(chip, 1, mate, 1).wait_recv()
    both = jnp.sum(chip[...] + recv[1], axis=1)
    s = jnp.concatenate([both, jnp.zeros((6, C), F32)], axis=0)
    lane = lax.broadcasted_iota(jnp.int32, s.shape, 1)
    for d in (1, 2, 4):
        s = s + jnp.where((lane & d) == 0, pltpu.roll(s, C - d, 1), pltpu.roll(s, d, 1))
    mean = s[0:1] / cnt
    inv = lax.rsqrt(s[1:2] / cnt - mean * mean + EPS)
    gn_ref[...] = jnp.zeros_like(gn_ref)
    gn_ref[0:1, :] = mean
    gn_ref[1:2, :] = inv * gamma_ref[gi:gi + 1, :]
    gn_ref[2:3, :] = beta_ref[gi:gi + 1, :]


def stats(sts, gamma, beta, gi, cnt, drop=False):
    part = pltpu.VMEM((2, 8, C), F32)
    return pl.pallas_call(
        functools.partial(stats_body, len(sts), gi, float(cnt), drop),
        in_specs=[VMEM] * (len(sts) + 2),
        out_specs=VMEM,
        out_shape=sds(8, C, dtype=F32),
        scratch_shapes=[part, part, pltpu.VMEM((2, 2, 8, C), F32), pltpu.SemaphoreType.DMA((3,)), pltpu.SemaphoreType.DMA((2,))],
        compiler_params=pltpu.CompilerParams(collective_id=gi, has_side_effects=True),
        name=f"stats_{gi}",
    )(*sts, gamma, beta)


def solution(mesh):
    nt = mesh.shape['t']
    send = lambda x: lax.ppermute(x, 't', [(i, i + 1) for i in range(nt - 1)])

    def local(z, w, b, gamma, beta):
        first = (lax.axis_index('t') == 0).astype(jnp.int32).reshape(1)
        w27 = w.reshape(-1, TAPS, C, C)
        cnt1 = nt * z.size // GROUPS
        cnt2 = (2 * 2 * nt - 1) * 4 * z.size // (2 * GROUPS)
        run = lambda frames, gn, wi, **kw: conv(frames, w27, b, gn, first, wi, **kw)
        tie = lambda x, y: lax.optimization_barrier((x, y))[0]
        z0, z1, st = prep(z)
        zb = send(z1)
        za = send(tie(z0, zb))
        gn = stats([st], gamma, beta, 0, cnt1)
        h1, st1 = run([(zb, 0), (z0, 0), (z1, 0)], gn, 0, nsub=1)
        hb = send(h1)
        h0, st0 = run([(za, 0), (zb, 0), (z0, 0)], gn, 0, nsub=2)
        ha = send(tie(h0, hb))
        gn = stats([st0, st1], gamma, beta, 1, cnt1)
        x1, _ = run([(hb, 0), (h0, 0), (h1, 0)], gn, 1, nsub=1, res=z1)
        xh = send(x1)
        x0, _ = run([(ha, 0), (hb, 0), (h0, 0)], gn, 1, nsub=2, res=z0)
        u23, st23 = up_conv(x0, x1, w27, b, first, False)
        uh = send(tie(u23, xh))
        u01, st01 = up_conv(xh, x0, w27, b, first, True)
        gn = stats([st01, st23], gamma, beta, 2, cnt2, drop=True)
        pair = lambda lo, hi: [(lo, 0), (lo, 1), (hi, 0), (hi, 1)]
        h23, st23 = run(pair(u01, u23), gn, 3)
        hh = send(h23)
        h01, st01 = run(pair(uh, u01), gn, 3, nsub=2)
        gn = stats([st01, st23], gamma, beta, 3, cnt2, drop=True)
        y = run(pair(h01, h23), gn, 4, res=u23, natural=True)
        return run(pair(hh, h01), gn, 4, nsub=2, res=u01, natural=True, ybuf=y)

    spec = P(('batch', 't'))
    return jax.shard_map(local, mesh=mesh, in_specs=(spec, P(), P(), P(), P()), out_specs=spec, check_vma=False)
```

time: 1190 us -> 454 us (0.38)
  matrix products: 473 us -> 0 us
  Pallas kernels: 0 us -> 425 us
  local copies, waits for them, and re-layouts: 347 us -> 1.97 us
  waiting for transfers between devices: 230 us -> 8.03 us
  other arithmetic: 99.3 us -> 0 us
  blocking collectives: 23.7 us -> 0 us
    conv_general_dilated x5 -> x0, matrix products: 473 us -> none  [conv_full(): lax.conv_general_dilated(xp[None], wk, (1, 1, 1), ((0, 0), (1, 1), (1, 1)...]
    pallas_call x0 -> x15, Pallas kernels: none -> 425 us  [the longest x8 340 us: conv(): pl.pallas_call(functools.partial(conv_body, H, J, R, wi, nf, nsub, res is...]
    ppermute x5 -> x7, waiting for transfers between devices: 230 us -> 8.03 us  [solution(): send = lambda x: lax.ppermute(x, 't', [(i, i + 1) for i in range(nt - 1)])]
    conv_general_dilated x16 -> x0, local copies, waits for them, and re-layouts: 206 us -> none  [conv_full(): lax.conv_general_dilated(xp[None], wk, (1, 1, 1), ((0, 0), (1, 1), (1, 1)...]
    convert_element_type x6 -> x0, other arithmetic: 70.2 us -> none  [the longest x4 40.6 us: gn_act(): jax.nn.silu(xn.astype(jnp.bfloat16).astype(jnp.float32))]
    broadcast_in_dim x11 -> x0, local copies, waits for them, and re-layouts: 58.7 us -> none  [the longest x3 27.2 us: local(): up = jnp.repeat(jnp.repeat(jnp.repeat(hx, 2, axis=0), 2, axis=1), 2, axis=2)]
    psum x4 -> x0, blocking collectives: 23.7 us -> none  [gn_act(): s = lax.psum(jnp.stack([s1, s2]), 't')]
    slice x6 -> x0, local copies, waits for them, and re-layouts: 22.1 us -> none  [the longest x3 17.8 us: from_prev(): got = lax.ppermute(x[-k:], 't', perm)]
  transfers between devices with their start and end apart: 5 -> 7, of which waited for: 5 -> 1; matrix products, arithmetic and copies ran while one was open for 2% -> 0% of each run, Pallas kernels for 0% -> 77%
where the time goes in v1:
time: 454 us; the launch traced here: 451 us
  Pallas kernels  425 us (94%)
  starting transfers between devices  15.1 us (3%)
  waiting for transfers between devices  8.03 us (2%)
    pallas_call x8, Pallas kernels, conv(): pl.pallas_call(functools.partial(conv_body, H, J, R, wi, nf, nsub, res is...  340 us
    pallas_call x2, Pallas kernels, up_conv(): pl.pallas_call(functools.partial(up_body, from_halo), grid=(HU // 4 + 2,)...  50.2 us
    pallas_call x4, Pallas kernels, stats(): pl.pallas_call(functools.partial(stats_body, len(sts), gi, float(cnt), dr...  31.1 us
    ppermute x7, starting transfers between devices, solution(): send = lambda x: lax.ppermute(x, 't', [(i, i + 1) for i in range(nt - 1)])  15.1 us
  transfers between devices with their start and end apart: 7, of which 1 were waited for; matrix products, arithmetic and copies ran while one was open for 0% of the time, Pallas kernels for 77%

profile of v1, /device:TPU:6, one launch (start us, length us, event | category | flops | bytes accessed | tf_op | source)
XLA Modules:
  0.0 450.6 jit_solution(1209433153731575258)
XLA Ops:
  0.0 4.0 prep.1
  4.0 1.9 collective-permute-start
  5.9 6.5 %stats_0.1.refs_1_ = f32[8,256]{1,0:T(8,128)} custom-call(f32[2,2,8,256]{3,2,1,0:T(8,128)} %get-tuple-element.25.refs_0_, f32[4,256]{1,0:T(4,128)} %refs_2_.21, f32[4,256]{1,0:T(4,128)} %refs_3_.5), custom_call_target="tpu_custom_call" | custom-call | tf_op jit(solution)/shard_map/stats_0/pallas_call | solution.py:505
  12.4 8.0 %collective-permute-done.refs_4_.refs_3_ = bf16[1,32,4,16,256]{4,3,2,1,0:T(8,128)(2,1)S(1)} collective-permute-done((bf16[1,32,4,16,256]{4,3,2,1,0:T(8,128)(2,1)}, bf16[1,32,4,16,256]{4,3,2,1,0:T(8,128)(2,1)S(1)}, u32[]{:S(2)}, u32[]{:S(2)}) %collective-permute-start) | collective-permute-done | bytes 1048608 | tf_op jit(solution)/shard_map/ppermute | solution.py:518
  20.4 1.9 collective-permute-start.1
  22.4 14.8 %conv0_11t.1 = (bf16[1,32,4,16,256]{4,3,2,1,0:T(8,128)(2,1)}, f32[1,2,8,256]{3,2,1,0:T(8,128)}) custom-call(s32[1]{0:T(128)} %bitcast.refs_0_.first_ref, f32[8,256]{1,0:T(8,128)} %stats_0.1.refs_1_, f32[5,256]{1,0:T(8,128)} %refs_2_.23, bf16[1,32,4,16,256]{4,3,2,1,0:T(8,128)(2,1)} %copy-done.1, ...), custom_call_target="tpu_custom_call" | custom-call | flops 7247757312 | bytes 3145728 | tf_op jit(solution)/shard_map/conv0_11t/pallas_call | solution.py:240
  37.2 1.9 collective-permute-start.2
  40.1 14.7 %conv0_12t.1 = (bf16[1,32,4,16,256]{4,3,2,1,0:T(8,128)(2,1)}, f32[1,2,8,256]{3,2,1,0:T(8,128)}) custom-call(s32[1]{0:T(128)} %bitcast.refs_0_.first_ref, f32[8,256]{1,0:T(8,128)} %stats_0.1.refs_1_, f32[5,256]{1,0:T(8,128)} %refs_2_.23, bf16[1,32,4,16,256]{4,3,2,1,0:T(8,128)(2,1)} %copy-done.4, bf16[1,32,4,16,256]{4,3,2,1,0:T(8,128)(2,1)} %copy-done.1, ...), custom_call_target="tpu_custom_call" | custom-call | flops 7247757312 | bytes 3145728 | tf_op jit(solution)/shard_map/conv0_12t/pallas_call | solution.py:240
  54.8 1.9 collective-permute-start.4
  56.8 7.2 %stats_1.1.refs_1_ = f32[8,256]{1,0:T(8,128)} custom-call(f32[1,2,8,256]{3,2,1,0:T(8,128)} %get-tuple-element.29.refs_0_, f32[1,2,8,256]{3,2,1,0:T(8,128)} %get-tuple-element.30.refs_1_, f32[4,256]{1,0:T(4,128)} %refs_2_.21, f32[4,256]{1,0:T(4,128)} %refs_3_.5), custom_call_target="tpu_custom_call" | custom-call | tf_op jit(solution)/shard_map/stats_1/pallas_call | solution.py:505
  64.0 15.2 %conv1_11t.1 = (bf16[1,32,4,16,256]{4,3,2,1,0:T(8,128)(2,1)}, f32[1,2,8,256]{3,2,1,0:T(8,128)}) custom-call(s32[1]{0:T(128)} %bitcast.refs_0_.first_ref, f32[8,256]{1,0:T(8,128)} %stats_1.1.refs_1_, f32[5,256]{1,0:T(8,128)} %refs_2_.23, bf16[1,32,4,16,256]{4,3,2,1,0:T(8,128)(2,1)} %copy-done, bf16[1,32,4,16,256]{4,3,2,1,0:T(8,128)(2,1)} %get-tuple-element.34.refs_4_.refs_5_, ...), custom_call_target="tpu_custom_call" | custom-call | flops 7247757312 | bytes 3145728 | tf_op jit(solution)/shard_map/conv1_11t/pallas_call | solution.py:240
  79.1 2.6 collective-permute-start.3
  81.7 1.0 copy-done.3
  82.7 15.1 %conv1_12t.1 = (bf16[1,32,4,16,256]{4,3,2,1,0:T(8,128)(2,1)}, f32[1,2,8,256]{3,2,1,0:T(8,128)}) custom-call(s32[1]{0:T(128)} %bitcast.refs_0_.first_ref, f32[8,256]{1,0:T(8,128)} %stats_1.1.refs_1_, f32[5,256]{1,0:T(8,128)} %refs_2_.23, bf16[1,32,4,16,256]{4,3,2,1,0:T(8,128)(2,1)} %copy-done.3, bf16[1,32,4,16,256]{4,3,2,1,0:T(8,128)(2,1)} %copy-done, ...), custom_call_target="tpu_custom_call" | custom-call | flops 7247757312 | bytes 3145728 | tf_op jit(solution)/shard_map/conv1_12t/pallas_call | solution.py:240
  97.9 25.1 %up.1 = (bf16[2,64,8,16,256]{4,3,2,1,0:T(8,128)(2,1)}, f32[2,2,8,256]{3,2,1,0:T(8,128)}) custom-call(s32[1]{0:T(128)} %bitcast.refs_0_.first_ref, f32[5,256]{1,0:T(8,128)} %refs_2_.23, bf16[1,32,4,16,256]{4,3,2,1,0:T(8,128)(2,1)} %get-tuple-element.35.xb_ref.xa_ref, bf16[1,32,4,16,256]{4,3,2,1,0:T(8,128)(2,1)} %get-tuple-element.33.xb_ref, ...), custom_call_target="tpu_custom_call" | custom-call | flops 7247757312 | bytes 5242880 | tf_op jit(solution)/shard_map/up/pallas_call | solution.py:401
  122.9 2.1 collective-permute-start.5
  125.1 25.1 %uph.1 = (bf16[2,64,8,16,256]{4,3,2,1,0:T(8,128)(2,1)}, f32[2,2,8,256]{3,2,1,0:T(8,128)}) custom-call(s32[1]{0:T(128)} %bitcast.refs_0_.first_ref, f32[5,256]{1,0:T(8,128)} %refs_2_.23, bf16[1,32,4,16,256]{4,3,2,1,0:T(8,128)(2,1)} %copy-done.2, bf16[1,32,4,16,256]{4,3,2,1,0:T(8,128)(2,1)} %get-tuple-element.35.xb_ref.xa_ref, bf16[5,27,256,256]{3,2,1,0:T(8,128)(2,1)} %bitcast.7), custom_call_target="tpu_custom_call" | custom-call | flops 7247757312 | bytes 5242880 | tf_op jit(solution)/shard_map/uph/pallas_call | solution.py:401
  150.2 9.3 %stats_2.1.refs_1_ = f32[8,256]{1,0:T(8,128)} custom-call(f32[2,2,8,256]{3,2,1,0:T(8,128)} %get-tuple-element.36.refs_0_, f32[2,2,8,256]{3,2,1,0:T(8,128)} %get-tuple-element.37.refs_1_, f32[4,256]{1,0:T(4,128)} %refs_2_.21, f32[4,256]{1,0:T(4,128)} %refs_3_.5), custom_call_target="tpu_custom_call" | custom-call | tf_op jit(solution)/shard_map/stats_2/pallas_call | solution.py:505
  159.5 68.0 %conv3_20t.1 = (bf16[2,64,8,16,256]{4,3,2,1,0:T(8,128)(2,1)}, f32[2,2,8,256]{3,2,1,0:T(8,128)}) custom-call(s32[1]{0:T(128)} %bitcast.refs_0_.first_ref, f32[8,256]{1,0:T(8,128)} %stats_2.1.refs_1_, f32[5,256]{1,0:T(8,128)} %refs_2_.23, bf16[2,64,8,16,256]{4,3,2,1,0:T(8,128)(2,1)} %get-tuple-element.40.refs_5_.refs_6_.refs_3_.refs_4_.refs_8_, ...), custom_call_target="tpu_custom_call" | custom-call | flops 57982058496 | bytes 25165824 | tf_op jit(solution)/shard_map/conv3_20t/pallas_call | solution.py:240
  227.5 2.7 collective-permute-start.6
  230.3 69.1 %conv3_22t.1 = (bf16[2,64,8,16,256]{4,3,2,1,0:T(8,128)(2,1)}, f32[2,2,8,256]{3,2,1,0:T(8,128)}) custom-call(s32[1]{0:T(128)} %bitcast.refs_0_.first_ref, f32[8,256]{1,0:T(8,128)} %stats_2.1.refs_1_, f32[5,256]{1,0:T(8,128)} %refs_2_.23, bf16[2,64,8,16,256]{4,3,2,1,0:T(8,128)(2,1)} %collective-permute-done.5.refs_3_.refs_4_, ...), custom_call_target="tpu_custom_call" | custom-call | flops 57982058496 | bytes 25165824 | tf_op jit(solution)/shard_map/conv3_22t/pallas_call | solution.py:240
  299.3 8.1 %stats_3.1.refs_1_ = f32[8,256]{1,0:T(8,128)} custom-call(f32[2,2,8,256]{3,2,1,0:T(8,128)} %get-tuple-element.41.refs_0_, f32[2,2,8,256]{3,2,1,0:T(8,128)} %get-tuple-element.42.refs_1_, f32[4,256]{1,0:T(4,128)} %refs_2_.21, f32[4,256]{1,0:T(4,128)} %refs_3_.5), custom_call_target="tpu_custom_call" | custom-call | tf_op jit(solution)/shard_map/stats_3/pallas_call | solution.py:505
  307.4 71.0 %conv4_20n.1.refs_9_ = bf16[4,64,128,256]{3,2,1,0:T(8,128)(2,1)} custom-call(s32[1]{0:T(128)} %bitcast.refs_0_.first_ref, f32[8,256]{1,0:T(8,128)} %stats_3.1.refs_1_, f32[5,256]{1,0:T(8,128)} %refs_2_.23, bf16[2,64,8,16,256]{4,3,2,1,0:T(8,128)(2,1)} %get-tuple-element.44.refs_3_.refs_4_.refs_5_.refs_6_, ...), custom_call_target="tpu_custom_call" | custom-call | flops 57982058496 | bytes 25165824 | tf_op jit(solution)/shard_map/conv4_20n/pallas_call | solution.py:240
  378.3 72.2 %conv4_22n.1 = bf16[4,64,128,256]{3,2,1,0:T(8,128)(2,1)} custom-call(s32[1]{0:T(128)} %bitcast.refs_0_.first_ref, f32[8,256]{1,0:T(8,128)} %stats_3.1.refs_1_, f32[5,256]{1,0:T(8,128)} %refs_2_.23, bf16[2,64,8,16,256]{4,3,2,1,0:T(8,128)(2,1)} %collective-permute-done.6.refs_3_.refs_4_, ...), custom_call_target="tpu_custom_call", output_to_operand_aliasing={{}: (9, {})} | custom-call | flops 57982058496 | bytes 25165824 | tf_op jit(solution)/shard_map/conv4_22n/pallas_call | solution.py:240
  (15 shorter events, 1.0 us)
Async XLA Ops:
  4.0 16.5 %collective-permute-start = (bf16[1,32,4,16,256]{4,3,2,1,0:T(8,128)(2,1)}, bf16[1,32,4,16,256]{4,3,2,1,0:T(8,128)(2,1)S(1)}, u32[]{:S(2)}, u32[]{:S(2)}) collective-permute-start(bf16[1,32,4,16,256]{4,3,2,1,0:T(8,128)(2,1)} %get-tuple-element.27.refs_5_.refs_7_), channel_id=1, source_target_pairs={{0,1},{1,2},{2,3},{4,5},{5,6},{6,7}} | collective-permute-start | bytes 3145736 | tf_op jit(solution)/shard_map/ppermute | solution.py:518
  20.4 1.9 copy-start.1
  20.4 18.7 %collective-permute-start.1 = (bf16[1,32,4,16,256]{4,3,2,1,0:T(8,128)(2,1)}, bf16[1,32,4,16,256]{4,3,2,1,0:T(8,128)(2,1)S(1)}, u32[]{:S(2)}, u32[]{:S(2)}) collective-permute-start(bf16[1,32,4,16,256]{4,3,2,1,0:T(8,128)(2,1)} %get-tuple-element.28.refs_5_.refs_4_.refs_7_), channel_id=1, source_target_pairs={{0,1},{1,2},{2,3},{4,5},{5,6},{6,7}} | collective-permute-start | bytes 3145736 | tf_op jit(solution)/shard_map/ppermute | solution.py:518
  37.2 17.6 %collective-permute-start.2 = (bf16[1,32,4,16,256]{4,3,2,1,0:T(8,128)(2,1)}, bf16[1,32,4,16,256]{4,3,2,1,0:T(8,128)(2,1)S(1)}, u32[]{:S(2)}, u32[]{:S(2)}) collective-permute-start(bf16[1,32,4,16,256]{4,3,2,1,0:T(8,128)(2,1)} %get-tuple-element.31.refs_5_), channel_id=1, source_target_pairs={{0,1},{1,2},{2,3},{4,5},{5,6},{6,7}} | collective-permute-start | bytes 3145736 | tf_op jit(solution)/shard_map/ppermute | solution.py:518
  39.1 1.0 copy-start.4
  54.8 9.1 %copy-start = (bf16[1,32,4,16,256]{4,3,2,1,0:T(8,128)(2,1)}, bf16[1,32,4,16,256]{4,3,2,1,0:T(8,128)(2,1)S(1)}, u32[]{:S(2)}) copy-start(bf16[1,32,4,16,256]{4,3,2,1,0:T(8,128)(2,1)S(1)} %collective-permute-done.2.refs_3_.refs_4_) | copy-start | bytes 3145732
  54.8 26.9 %collective-permute-start.4 = (bf16[1,32,4,16,256]{4,3,2,1,0:T(8,128)(2,1)}, bf16[1,32,4,16,256]{4,3,2,1,0:T(8,128)(2,1)S(1)}, u32[]{:S(2)}, u32[]{:S(2)}) collective-permute-start(bf16[1,32,4,16,256]{4,3,2,1,0:T(8,128)(2,1)} %get-tuple-element.34.refs_4_.refs_5_), channel_id=1, source_target_pairs={{0,1},{1,2},{2,3},{4,5},{5,6},{6,7}} | collective-permute-start | bytes 3145736 | tf_op jit(solution)/shard_map/ppermute | solution.py:518
  79.1 43.8 %collective-permute-start.3 = (bf16[1,32,4,16,256]{4,3,2,1,0:T(8,128)(2,1)}, bf16[1,32,4,16,256]{4,3,2,1,0:T(8,128)(2,1)S(1)}, u32[]{:S(2)}, u32[]{:S(2)}) collective-permute-start(bf16[1,32,4,16,256]{4,3,2,1,0:T(8,128)(2,1)} %get-tuple-element.33.xb_ref), channel_id=1, source_target_pairs={{0,1},{1,2},{2,3},{4,5},{5,6},{6,7}} | collective-permute-start | bytes 3145736 | tf_op jit(solution)/shard_map/ppermute | solution.py:518
  81.7 1.0 copy-start.3
  122.9 2.2 copy-start.2
  122.9 107.3 %collective-permute-start.5 = (bf16[2,64,8,16,256]{4,3,2,1,0:T(8,128)(2,1)}, bf16[2,64,8,16,256]{4,3,2,1,0:T(8,128)(2,1)}, u32[]{:S(2)}, u32[]{:S(2)}) collective-permute-start(bf16[2,64,8,16,256]{4,3,2,1,0:T(8,128)(2,1)} %get-tuple-element.39.refs_5_.refs_6_.refs_8_), channel_id=1, source_target_pairs={{0,1},{1,2},{2,3},{4,5},{5,6},{6,7}} | collective-permute-start | bytes 25165832 | tf_op jit(solution)/shard_map/ppermute | solution.py:518
  227.5 150.8 %collective-permute-start.6 = (bf16[2,64,8,16,256]{4,3,2,1,0:T(8,128)(2,1)}, bf16[2,64,8,16,256]{4,3,2,1,0:T(8,128)(2,1)}, u32[]{:S(2)}, u32[]{:S(2)}) collective-permute-start(bf16[2,64,8,16,256]{4,3,2,1,0:T(8,128)(2,1)} %get-tuple-element.43.refs_5_.refs_6_), channel_id=1, source_target_pairs={{0,1},{1,2},{2,3},{4,5},{5,6},{6,7}} | collective-permute-start | bytes 25165832 | tf_op jit(solution)/shard_map/ppermute | solution.py:518

commit v2 on v1

--- a/solution.py
+++ b/solution.py
@@ -5,6 +5,7 @@
 from jax.experimental import pallas as pl
 from jax.experimental.pallas import tpu as pltpu
 from jax.sharding import PartitionSpec as P
+
 
 GROUPS = 32
 EPS = 1e-6
@@ -19,7 +20,12 @@
 MESH = pl.DeviceIdType.MESH
 SMEM = pl.BlockSpec(memory_space=pltpu.SMEM)
 VMEM = pl.BlockSpec(memory_space=pltpu.VMEM)
-PARAMS = pltpu.CompilerParams(vmem_limit_bytes=58 * 2**20)
+ANY = pl.BlockSpec(memory_space=pl.ANY)
+WEIGHTS = [pltpu.VMEM((TAPS, C, C), BF), pltpu.SemaphoreType.DMA]
+
+
+def params(mib):
+    return pltpu.CompilerParams(vmem_limit_bytes=mib * 2**20)
 
 
 def sds(*shape, dtype=BF):
@@ -71,14 +77,15 @@
     it = iter(refs)
     first_ref, gn_ref, b_ref = (next(it) for _ in range(3))
     frames = [next(it) for _ in range(nf)]
-    w_ref = next(it)
-    res_ref = next(it) if has_res else None
+    w_hbm = next(it)
+    res = [next(it) for _ in range(nf - 2)] if has_res else None
     if aliased:
         next(it)
     out_ref = next(it)
     st_ref = None if natural else next(it)
-    xs = next(it)
+    xs, w_ref, sem = (next(it) for _ in range(3))
     nat = next(it) if natural else None
+    weights = pltpu.make_async_copy(w_hbm.at[wi], w_ref, sem)
     HR = (5 - nf) * R
     nblk = H // (2 * HR)
     last = nblk + 1
@@ -104,6 +111,7 @@
                     xs[dst, J + 1] = shifted(s, False)
                 if j == J - 1:
                     xs[dst, 0] = shifted(s, True)
+
             return go
 
         def act_items(half):
@@ -115,6 +123,7 @@
                     for j in range(J):
                         act_item(f, r, j)()
                 return 0
+
             lax.fori_loop(0, jnp.where(t == 0, 2 * HR, HR), go, 0)
 
         def pop_item(acc, q, half, r, piece):
@@ -124,7 +133,7 @@
                 v = pltpu.matmul_pop(acc) + b_ref[wi:wi + 1, :]
                 ob = v.astype(BF)
                 if has_res:
-                    h = ob.astype(F32) + res_ref[of(q), row, tiles].astype(F32).reshape(PT * S, C)
+                    h = ob.astype(F32) + res[of(q)][0, row, tiles].astype(F32).reshape(PT * S, C)
                     ob = h.astype(BF)
                 if natural:
                     for k in range(PT):
@@ -136,6 +145,7 @@
                 else:
                     out_ref[of(q), row, tiles] = ob.reshape(PT, S, C)
                     add_sums(st_ref, of(q), ob)
+
             return go
 
         def pops(accs, half):
@@ -151,9 +161,10 @@
                     lhs = xs[(of(q) + kt) * HP + y0 + orow(q, r) + kh, pl.ds(kw + p * PT, PT)].reshape(PT * S, C)
                     pltpu.matmul_acc_lhs(accs[q][r][p], lhs, load_staged_rhs=reg if lead else None)
                 if lead:
-                    nxt = w_ref[0, (n + 1) % TAPS]
+                    nxt = w_ref[(n + 1) % TAPS]
                     for q in PAIR:
                         pltpu.matmul_push_rhs(nxt, staging_register=1 - reg, mxu_index=q)
+
             return go
 
         def mxu_items(accs, y0, half):
@@ -166,6 +177,7 @@
 
         @pl.when(t == 0)
         def _():
+            weights.start()
             for accs in (accA, accB):
                 for q in PAIR:
                     for a in sum(accs[q], []):
@@ -184,17 +196,18 @@
 
         @pl.when(t >= 2)
         def _():
-            spread(mxu_items(accA, (t - 2) * (2 * HR) + HR, 0), pops(accB, 0) + act_items(0), 4)
+            spread(mxu_items(accA, (t - 2) * (2 * HR) + HR, 0), pops(accB, 0) + act_items(0), 0)
 
         @pl.when(t == 0)
         def _():
             dummy()
+            weights.wait()
             for q in PAIR:
-                pltpu.matmul_push_rhs(w_ref[0, 0], staging_register=1, mxu_index=q)
+                pltpu.matmul_push_rhs(w_ref[0], staging_register=1, mxu_index=q)
 
         @pl.when((t >= 1) & (t < last))
         def _():
-            spread(mxu_items(accB, (t - 1) * (2 * HR), 1), pops(accA, 1) + act_items(1), 4)
+            spread(mxu_items(accB, (t - 1) * (2 * HR), 1), pops(accA, 1) + act_items(1), 0)
 
         @pl.when(t == last)
         def _():
@@ -206,6 +219,7 @@
         def step(u, _):
             half_steps(2 * pl.program_id(0) + u, u, *accs)
             return 0
+
         lax.fori_loop(0, 2, step, 0)
 
     acc = lambda q: [[pltpu.ACC(q)((PT * S, C), F32) for _ in range(NP)] for _ in range(R)]
@@ -222,16 +236,16 @@
     outi = lambda t: jnp.maximum(t - 1, 0)
     late = pl.BlockSpec((nout, rows, J, S, C), lambda t: (0, outi(t), 0, 0, 0))
     now = lambda k: pl.BlockSpec((1, rows, J, S, C), lambda t: (k, jnp.minimum(t, nst - 1), 0, 0, 0))
-    in_specs = [SMEM, whole(8, C), whole(5, C)] + [now(k) for _, k in frames] + [whole(1, TAPS, C, C, lead=wi)]
+    in_specs = [SMEM, whole(8, C), whole(5, C)] + [now(k) for _, k in frames] + [ANY]
     args = [first, gn, b] + [a for a, _ in frames] + [w27]
-    scratch = [pltpu.VMEM((nf * HP, J + 2, S, C), BF)]
-    if res is not None:
-        in_specs.append(late)
-        args.append(res)
+    scratch = [pltpu.VMEM((nf * HP, J + 2, S, C), BF)] + WEIGHTS
+    for a, k in res or ():
+        in_specs.append(pl.BlockSpec((1, rows, J, S, C), lambda t, k=k: (k, outi(t), 0, 0, 0)))
+        args.append(a)
     if natural:
         fi = 1 if ybuf is None else 0
         if ybuf is not None:
-            in_specs.append(pl.BlockSpec(memory_space=pl.ANY))
+            in_specs.append(ANY)
             args.append(ybuf)
         oshape, ospec = sds(2 * nout, H, J * S, C), pl.BlockSpec((nout, rows, J * S, C), lambda t: (fi, outi(t), 0, 0))
         scratch.append(pltpu.VMEM((R, 2, 2, J * S, LANES), F32))
@@ -245,9 +259,8 @@
         out_shape=oshape,
         input_output_aliases={} if ybuf is None else {len(args) - 1: 0},
         scratch_shapes=scratch,
-        compiler_params=PARAMS,
+        compiler_params=params(46 if H == HU else 61),
         cost_estimate=cost(2 * nout * H * J * S * TAPS * C * C, 6 * nout * H * J * S * C),
-        name=f"conv{wi}_{nout}{nsub}" + ("n" if natural else "t"),
     )(*args)
 
 
@@ -257,19 +270,23 @@
        for kt in range(kind[0], 3 - kind[0], 2) for kh in range(kind[1], 3 - kind[1], 2) for kw in range(kind[2], 3 - kind[2], 2)]
 
 
-def up_body(from_halo, first_ref, b_ref, xa_ref, xb_ref, w_ref, u_ref, st_ref, xs, es):
+def up_body(from_halo, first_ref, b_ref, xa_ref, xb_ref, w_hbm, u_ref, st_ref, xs, es, w_ref, sem):
     t = pl.program_id(0)
     last = HU // 4 + 1
     slots = [lax.rem(t + k, NS) for k in range(NS)]
+    weights = pltpu.make_async_copy(w_hbm.at[2], w_ref, sem)
 
     def fill(f, src):
-        def go(r, _):
-            row = f * HPU + PADR + r
-            xs[row, 1:JU + 1] = src[0, r]
-            xs[row, JU + 1] = shifted(src[0, r, 0].astype(F32), False)
-            xs[row, 0] = shifted(src[0, r, JU - 1].astype(F32), True)
+        def go(i, _):
+            for r in range(8):
+                r = i * 8 + r
+                row = f * HPU + PADR + r
+                xs[row, 1:JU + 1] = src[0, r]
+                xs[row, JU + 1] = shifted(src[0, r, 0].astype(F32), False)
+                xs[row, 0] = shifted(src[0, r, JU - 1].astype(F32), True)
             return 0
-        lax.fori_loop(0, HU, go, 0)
+
+        lax.fori_loop(0, HU // 8, go, 0)
 
     def mxu_items(accE, accF):
         def tiles_of(n):
@@ -277,13 +294,13 @@
             return (accF, JU, JU + 1) if ww else (accE[n // 2 % 2], JU + 1, 0)
 
         def push(k):
-            w = w_ref[0, SEQ[k][1] * 9 + SEQ[k][2] * 3 + SEQ[k][3]]
+            w = w_ref[SEQ[k][1] * 9 + SEQ[k][2] * 3 + SEQ[k][3]]
             for q in PAIR:
                 pltpu.matmul_push_rhs(w, staging_register=k % 2, mxu_index=q)
 
         def acc_item(k):
             n, kt, kh, kw = SEQ[k]
-            tt, hh, ww = KINDS[n]
+            tt, hh, _ = KINDS[n]
             refs, nt, _ = tiles_of(n)
             frames = PAIR if tt else (kt // 2,)
 
@@ -300,10 +317,11 @@
                         load = None
                     if f == frames[0] and k + 1 < TAPS:
                         push(k + 1)
+
             return go
 
         def pop_item(n):
-            tt, hh, ww = KINDS[n]
+            tt, hh, _ = KINDS[n]
             refs, nt, off = tiles_of(n)
 
             def go():
@@ -311,6 +329,7 @@
                     for i in PAIR:
                         for q in PAIR:
                             es[slots[0], q, tt + ai, hh, i, off:off + nt] = pltpu.matmul_pop(refs[q][2 * ai + i]).reshape(nt, S, C)
+
             return go
 
         items = []
@@ -354,6 +373,7 @@
             for p in PAIR:
                 for z in PAIR:
                     st_ref[p, z, :, cols] += tot[p][z]
+
         return go
 
     def body(accE, accF):
@@ -361,6 +381,7 @@
 
         @pl.when(t == 0)
         def _():
+            weights.start()
             for q in PAIR:
                 for a in accE[0][q] + accE[1][q] + accF[q]:
                     pltpu.matmul_pop(a)
@@ -378,6 +399,7 @@
                     fill(0, xa_ref)
             else:
                 fill(0, xa_ref)
+            weights.wait()
 
         @pl.when(t == 2)
         def _():
@@ -396,18 +418,18 @@
     pl.run_scoped(body, [refs(JU + 1), refs(JU + 1)], refs(JU))
 
 
-def up_conv(xa, xb, w27, b, first, from_halo):
+def up_conv(a, c, w27, b, first, from_halo):
+    (xa, ka), (xb, kb) = a, c
     frame = (1, HU, JU, S, C)
     return pl.pallas_call(
         functools.partial(up_body, from_halo),
         grid=(HU // 4 + 2,),
-        in_specs=[SMEM, whole(5, C), whole(*frame), whole(*frame), whole(1, TAPS, C, C, lead=2)],
+        in_specs=[SMEM, whole(5, C), whole(*frame, lead=ka), whole(*frame, lead=kb), ANY],
         out_specs=[pl.BlockSpec((2, 8, 2 * JU, S, C), lambda t: (0, jnp.clip(t - 2, 0, HU // 4 - 1), 0, 0, 0)), whole(2, 2, 8, C)],
         out_shape=[sds(2, 2 * HU, 2 * JU, S, C), sds(2, 2, 8, C, dtype=F32)],
-        scratch_shapes=[pltpu.VMEM((2 * HPU, JU + 2, S, C), BF), pltpu.VMEM((NS, 2, 3, 2, 2, 2 * JU + 1, S, C), F32)],
-        compiler_params=PARAMS,
-        cost_estimate=cost(2 * xb.size * TAPS * C, 10 * xb.size),
-        name="up" + ("h" if from_halo else ""),
+        scratch_shapes=[pltpu.VMEM((2 * HPU, JU + 2, S, C), BF), pltpu.VMEM((NS, 2, 3, 2, 2, 2 * JU + 1, S, C), F32)] + WEIGHTS,
+        compiler_params=params(46),
+        cost_estimate=cost(4 * HU * JU * S * C * TAPS * C, 10 * HU * JU * S * C),
     )(first, b, xa, xb, w27)
 
 
@@ -437,7 +459,7 @@
         out_specs=[pl.BlockSpec((1, rows, JU, S, C), lambda t: (0, t, 0, 0, 0))] * 2 + [whole(2, 2, 8, C)],
         out_shape=[sds(1, HU, JU, S, C)] * 2 + [sds(2, 2, 8, C, dtype=F32)],
         scratch_shapes=[pltpu.VMEM((2, rows, 2, width, LANES), F32)],
-        compiler_params=PARAMS,
+        compiler_params=params(46),
         cost_estimate=cost(8 * z.size, 4 * z.size),
         name="prep",
     )(z)
@@ -508,14 +530,17 @@
         out_specs=VMEM,
         out_shape=sds(8, C, dtype=F32),
         scratch_shapes=[part, part, pltpu.VMEM((2, 2, 8, C), F32), pltpu.SemaphoreType.DMA((3,)), pltpu.SemaphoreType.DMA((2,))],
-        compiler_params=pltpu.CompilerParams(collective_id=gi, has_side_effects=True),
-        name=f"stats_{gi}",
+        compiler_params=pltpu.CompilerParams(collective_id=gi, has_side_effects=True, vmem_limit_bytes=46 * 2**20),
     )(*sts, gamma, beta)
 
 
 def solution(mesh):
     nt = mesh.shape['t']
-    send = lambda x: lax.ppermute(x, 't', [(i, i + 1) for i in range(nt - 1)])
+
+    hbm = lambda x: pltpu.with_memory_space_constraint(x, pltpu.HBM)
+
+    def send(x):
+        return lax.ppermute(x, 't', [(i, i + 1) for i in range(nt - 1)])
 
     def local(z, w, b, gamma, beta):
         first = (lax.axis_index('t') == 0).astype(jnp.int32).reshape(1)
@@ -523,30 +548,30 @@
         cnt1 = nt * z.size // GROUPS
         cnt2 = (2 * 2 * nt - 1) * 4 * z.size // (2 * GROUPS)
         run = lambda frames, gn, wi, **kw: conv(frames, w27, b, gn, first, wi, **kw)
-        tie = lambda x, y: lax.optimization_barrier((x, y))[0]
-        z0, z1, st = prep(z)
+        z0, z1, st = prep(hbm(z))
         zb = send(z1)
-        za = send(tie(z0, zb))
+        za = send(z0)
         gn = stats([st], gamma, beta, 0, cnt1)
         h1, st1 = run([(zb, 0), (z0, 0), (z1, 0)], gn, 0, nsub=1)
         hb = send(h1)
         h0, st0 = run([(za, 0), (zb, 0), (z0, 0)], gn, 0, nsub=2)
-        ha = send(tie(h0, hb))
+        ha = send(h0)
         gn = stats([st0, st1], gamma, beta, 1, cnt1)
-        x1, _ = run([(hb, 0), (h0, 0), (h1, 0)], gn, 1, nsub=1, res=z1)
+        x1, _ = run([(hb, 0), (h0, 0), (h1, 0)], gn, 1, nsub=1, res=[(z1, 0)])
         xh = send(x1)
-        x0, _ = run([(ha, 0), (hb, 0), (h0, 0)], gn, 1, nsub=2, res=z0)
-        u23, st23 = up_conv(x0, x1, w27, b, first, False)
-        uh = send(tie(u23, xh))
-        u01, st01 = up_conv(xh, x0, w27, b, first, True)
+        x0, _ = run([(ha, 0), (hb, 0), (h0, 0)], gn, 1, nsub=2, res=[(z0, 0)])
+        u23, st23 = up_conv((x0, 0), (x1, 0), w27, b, first, False)
+        uh = send(u23)
+        u01, st01 = up_conv((xh, 0), (x0, 0), w27, b, first, True)
         gn = stats([st01, st23], gamma, beta, 2, cnt2, drop=True)
         pair = lambda lo, hi: [(lo, 0), (lo, 1), (hi, 0), (hi, 1)]
         h23, st23 = run(pair(u01, u23), gn, 3)
         hh = send(h23)
         h01, st01 = run(pair(uh, u01), gn, 3, nsub=2)
         gn = stats([st01, st23], gamma, beta, 3, cnt2, drop=True)
-        y = run(pair(h01, h23), gn, 4, res=u23, natural=True)
-        return run(pair(hh, h01), gn, 4, nsub=2, res=u01, natural=True, ybuf=y)
+        y = run(pair(h01, h23), gn, 4, res=[(u23, 0), (u23, 1)], natural=True)
+        return run(pair(hh, h01), gn, 4, nsub=2, res=[(u01, 0), (u01, 1)], natural=True, ybuf=y)
 
     spec = P(('batch', 't'))
+
     return jax.shard_map(local, mesh=mesh, in_specs=(spec, P(), P(), P(), P()), out_specs=spec, check_vma=False)

time: 454 us -> 533 us (1.17)
  waiting for transfers between devices: 8.03 us -> 107 us
  Pallas kernels: 425 us -> 403 us
    ppermute x7, waiting for transfers between devices: 8.03 us -> 107 us  [send(): return lax.ppermute(x, 't', [(i, i + 1) for i in range(nt - 1)])]
    pallas_call x8, Pallas kernels: 340 us -> 330 us  [conv(): pl.pallas_call(functools.partial(conv_body, H, J, R, wi, nf, nsub, res is...]
    pallas_call x4, Pallas kernels: 31.1 us -> 23.7 us  [stats(): pl.pallas_call(functools.partial(stats_body, len(sts), gi, float(cnt), dr...]
  transfers between devices with their start and end apart: 7 -> 7, of which waited for: 1 -> 2; matrix products, arithmetic and copies ran while one was open for 0% -> 0% of each run, Pallas kernels for 77% -> 55%
where the time goes in v2:
time: 533 us; the launch traced here: 529 us
  Pallas kernels  403 us (76%)
  waiting for transfers between devices  107 us (20%)
  starting transfers between devices  14.7 us (3%)
    pallas_call x8, Pallas kernels, conv(): pl.pallas_call(functools.partial(conv_body, H, J, R, wi, nf, nsub, res is...  330 us
    ppermute x7, waiting for transfers between devices, send(): return lax.ppermute(x, 't', [(i, i + 1) for i in range(nt - 1)])  107 us
    pallas_call x2, Pallas kernels, up_conv(): pl.pallas_call(functools.partial(up_body, from_halo), grid=(HU // 4 + 2,)...  47.5 us
    pallas_call x4, Pallas kernels, stats(): pl.pallas_call(functools.partial(stats_body, len(sts), gi, float(cnt), dr...  23.7 us
    ppermute x7, starting transfers between devices, send(): return lax.ppermute(x, 't', [(i, i + 1) for i in range(nt - 1)])  14.7 us
  transfers between devices with their start and end apart: 7, of which 2 were waited for; matrix products, arithmetic and copies ran while one was open for 0% of the time, Pallas kernels for 55%

profile of v2, /device:TPU:6, one launch (start us, length us, event | category | flops | bytes accessed | tf_op | source)
XLA Modules:
  0.0 529.3 jit_solution(9117614798329124110)
XLA Ops:
  0.0 2.8 prep.1
  2.8 1.9 collective-permute-start.1
  4.7 1.9 collective-permute-start
  8.0 6.5 %shard_map.55.refs_1_ = f32[8,256]{1,0:T(8,128)S(1)} custom-call(f32[2,2,8,256]{3,2,1,0:T(8,128)S(1)} %get-tuple-element.22.refs_0_, f32[4,256]{1,0:T(4,128)S(1)} %copy-done, f32[4,256]{1,0:T(4,128)S(1)} %copy-done.2), custom_call_target="tpu_custom_call" | custom-call | tf_op jit(solution)/shard_map/pallas_call | solution.py:527
  14.5 4.9 collective-permute-done.1.refs_4_.refs_3_
  20.0 13.0 %shard_map.57 = (bf16[1,32,4,16,256]{4,3,2,1,0:T(8,128)(2,1)S(1)}, f32[1,2,8,256]{3,2,1,0:T(8,128)S(1)}) custom-call(s32[1]{0:T(128)} %bitcast.refs_0_.first_ref, f32[8,256]{1,0:T(8,128)S(1)} %shard_map.55.refs_1_, f32[5,256]{1,0:T(8,128)S(1)} %copy-done.8, bf16[1,32,4,16,256]{4,3,2,1,0:T(8,128)(2,1)} %collective-permute-done.1.refs_4_.refs_3_, ...), custom_call_target="tpu_custom_call" | custom-call | flops 7247757312 | bytes 3145728 | tf_op jit(solution)/shard_map/pallas_call | solution.py:254
  33.0 1.9 collective-permute-start.2
  35.0 13.6 %shard_map.56 = (bf16[1,32,4,16,256]{4,3,2,1,0:T(8,128)(2,1)S(1)}, f32[1,2,8,256]{3,2,1,0:T(8,128)S(1)}) custom-call(s32[1]{0:T(128)} %bitcast.refs_0_.first_ref, f32[8,256]{1,0:T(8,128)S(1)} %shard_map.55.refs_1_, f32[5,256]{1,0:T(8,128)S(1)} %copy-done.9, bf16[1,32,4,16,256]{4,3,2,1,0:T(8,128)(2,1)} %collective-permute-done.refs_3_, ...), custom_call_target="tpu_custom_call" | custom-call | flops 7247757312 | bytes 3145728 | tf_op jit(solution)/shard_map/pallas_call | solution.py:254
  48.6 2.1 collective-permute-start.4
  50.8 6.4 %shard_map.58.refs_1_ = f32[8,256]{1,0:T(8,128)S(1)} custom-call(f32[1,2,8,256]{3,2,1,0:T(8,128)S(1)} %get-tuple-element.25.refs_0_, f32[1,2,8,256]{3,2,1,0:T(8,128)S(1)} %get-tuple-element.26.refs_1_, f32[4,256]{1,0:T(4,128)S(1)} %copy-done.1, f32[4,256]{1,0:T(4,128)S(1)} %copy-done.3), custom_call_target="tpu_custom_call" | custom-call | tf_op jit(solution)/shard_map/pallas_call | solution.py:527
  57.2 12.7 %shard_map.59 = (bf16[1,32,4,16,256]{4,3,2,1,0:T(8,128)(2,1)S(1)}, f32[1,2,8,256]{3,2,1,0:T(8,128)}) custom-call(s32[1]{0:T(128)} %bitcast.refs_0_.first_ref, f32[8,256]{1,0:T(8,128)S(1)} %shard_map.58.refs_1_, f32[5,256]{1,0:T(8,128)S(1)} %copy-done.9, bf16[1,32,4,16,256]{4,3,2,1,0:T(8,128)(2,1)S(1)} %collective-permute-done.2.refs_3_.refs_4_, ...), custom_call_target="tpu_custom_call" | custom-call | flops 7247757312 | bytes 3145728 | tf_op jit(solution)/shard_map/pallas_call | solution.py:254
  69.9 13.1 %shard_map.60 = (bf16[1,32,4,16,256]{4,3,2,1,0:T(8,128)(2,1)S(1)}, f32[1,2,8,256]{3,2,1,0:T(8,128)}) custom-call(s32[1]{0:T(128)} %bitcast.refs_0_.first_ref, f32[8,256]{1,0:T(8,128)S(1)} %shard_map.58.refs_1_, f32[5,256]{1,0:T(8,128)S(1)} %copy-done.9, bf16[1,32,4,16,256]{4,3,2,1,0:T(8,128)(2,1)S(1)} %collective-permute-done.4.refs_3_, ...), custom_call_target="tpu_custom_call" | custom-call | flops 7247757312 | bytes 3145728 | tf_op jit(solution)/shard_map/pallas_call | solution.py:254
  83.0 23.8 %shard_map.62 = (bf16[2,64,8,16,256]{4,3,2,1,0:T(8,128)(2,1)}, f32[2,2,8,256]{3,2,1,0:T(8,128)S(1)}) custom-call(s32[1]{0:T(128)} %bitcast.refs_0_.first_ref, f32[5,256]{1,0:T(8,128)S(1)} %copy-done.9, bf16[1,32,4,16,256]{4,3,2,1,0:T(8,128)(2,1)S(1)} %get-tuple-element.30.xb_ref.xa_ref, bf16[1,32,4,16,256]{4,3,2,1,0:T(8,128)(2,1)S(1)} %get-tuple-element.29.xb_ref, ...), custom_call_target="tpu_custom_call" | custom-call | flops 14495514624 | bytes 5242880 | tf_op jit(solution)/shard_map/pallas_call | solution.py:424
  106.7 2.4 collective-permute-start.5
  109.1 2.1 collective-permute-start.3
  111.3 101.7 %collective-permute-done.3.xa_ref = bf16[1,32,4,16,256]{4,3,2,1,0:T(8,128)(2,1)S(1)} collective-permute-done((bf16[1,32,4,16,256]{4,3,2,1,0:T(8,128)(2,1)S(1)}, bf16[1,32,4,16,256]{4,3,2,1,0:T(8,128)(2,1)S(1)}, u32[]{:S(2)}, u32[]{:S(2)}) %collective-permute-start.3) | collective-permute-done | bytes 1048608 | tf_op jit(solution)/shard_map/ppermute | solution.py:543
  213.0 23.8 %shard_map.61 = (bf16[2,64,8,16,256]{4,3,2,1,0:T(8,128)(2,1)}, f32[2,2,8,256]{3,2,1,0:T(8,128)S(1)}) custom-call(s32[1]{0:T(128)} %bitcast.refs_0_.first_ref, f32[5,256]{1,0:T(8,128)S(1)} %copy-done.9, bf16[1,32,4,16,256]{4,3,2,1,0:T(8,128)(2,1)S(1)} %collective-permute-done.3.xa_ref, bf16[1,32,4,16,256]{4,3,2,1,0:T(8,128)(2,1)S(1)} %get-tuple-element.30.xb_ref.xa_ref, ...), custom_call_target="tpu_custom_call" | custom-call | flops 14495514624 | bytes 5242880 | tf_op jit(solution)/shard_map/pallas_call | solution.py:424
  236.7 4.9 shard_map.63.refs_1_
  242.2 66.8 %shard_map.65 = (bf16[2,64,8,16,256]{4,3,2,1,0:T(8,128)(2,1)}, f32[2,2,8,256]{3,2,1,0:T(8,128)}) custom-call(s32[1]{0:T(128)} %bitcast.refs_0_.first_ref, f32[8,256]{1,0:T(8,128)} %copy-done.6, f32[5,256]{1,0:T(8,128)} %refs_2_.23, bf16[2,64,8,16,256]{4,3,2,1,0:T(8,128)(2,1)} %get-tuple-element.34.refs_5_.refs_6_.refs_3_.refs_4_.refs_8_.refs_9_, ...), custom_call_target="tpu_custom_call" | custom-call | flops 57982058496 | bytes 25165824 | tf_op jit(solution)/shard_map/pallas_call | solution.py:254
  309.0 2.3 collective-permute-start.6
  311.4 68.5 %shard_map.64 = (bf16[2,64,8,16,256]{4,3,2,1,0:T(8,128)(2,1)}, f32[2,2,8,256]{3,2,1,0:T(8,128)}) custom-call(s32[1]{0:T(128)} %bitcast.refs_0_.first_ref, f32[8,256]{1,0:T(8,128)} %copy-done.6, f32[5,256]{1,0:T(8,128)} %refs_2_.23, bf16[2,64,8,16,256]{4,3,2,1,0:T(8,128)(2,1)} %collective-permute-done.5.refs_3_.refs_4_, ...), custom_call_target="tpu_custom_call" | custom-call | flops 57982058496 | bytes 25165824 | tf_op jit(solution)/shard_map/pallas_call | solution.py:254
  380.6 5.9 %shard_map.66.refs_1_ = f32[8,256]{1,0:T(8,128)S(1)} custom-call(f32[2,2,8,256]{3,2,1,0:T(8,128)S(1)} %copy-done.5, f32[2,2,8,256]{3,2,1,0:T(8,128)S(1)} %copy-done.4, f32[4,256]{1,0:T(4,128)S(1)} %copy-done.1, f32[4,256]{1,0:T(4,128)S(1)} %copy-done.3), custom_call_target="tpu_custom_call" | custom-call | tf_op jit(solution)/shard_map/pallas_call | solution.py:527
  387.2 69.9 %shard_map.67.refs_10_ = bf16[4,64,128,256]{3,2,1,0:T(8,128)(2,1)} custom-call(s32[1]{0:T(128)} %bitcast.refs_0_.first_ref, f32[8,256]{1,0:T(8,128)} %copy-done.7, f32[5,256]{1,0:T(8,128)} %refs_2_.23, bf16[2,64,8,16,256]{4,3,2,1,0:T(8,128)(2,1)} %get-tuple-element.38.refs_3_.refs_4_.refs_5_.refs_6_, ...), custom_call_target="tpu_custom_call" | custom-call | flops 57982058496 | bytes 25165824 | tf_op jit(solution)/shard_map/pallas_call | solution.py:254
  457.1 72.0 %shard_map.68 = bf16[4,64,128,256]{3,2,1,0:T(8,128)(2,1)} custom-call(s32[1]{0:T(128)} %bitcast.refs_0_.first_ref, f32[8,256]{1,0:T(8,128)} %copy-done.7, f32[5,256]{1,0:T(8,128)} %refs_2_.23, bf16[2,64,8,16,256]{4,3,2,1,0:T(8,128)(2,1)} %collective-permute-done.6.refs_3_.refs_4_, ...), custom_call_target="tpu_custom_call", output_to_operand_aliasing={{}: (10, {})} | custom-call | flops 57982058496 | bytes 25165824 | tf_op jit(solution)/shard_map/pallas_call | solution.py:254
  (25 shorter events, 4.0 us)
Async XLA Ops:
  2.8 16.6 %collective-permute-start.1 = (bf16[1,32,4,16,256]{4,3,2,1,0:T(8,128)(2,1)S(1)}, bf16[1,32,4,16,256]{4,3,2,1,0:T(8,128)(2,1)}, u32[]{:S(2)}, u32[]{:S(2)}) collective-permute-start(bf16[1,32,4,16,256]{4,3,2,1,0:T(8,128)(2,1)S(1)} %get-tuple-element.24.refs_5_.refs_7_), channel_id=1, source_target_pairs={{0,1},{1,2},{2,3},{4,5},{5,6},{6,7}} | collective-permute-start | bytes 3145736 | tf_op jit(solution)/shard_map/ppermute | solution.py:543
  4.7 30.3 %collective-permute-start = (bf16[1,32,4,16,256]{4,3,2,1,0:T(8,128)(2,1)S(1)}, bf16[1,32,4,16,256]{4,3,2,1,0:T(8,128)(2,1)}, u32[]{:S(2)}, u32[]{:S(2)}) collective-permute-start(bf16[1,32,4,16,256]{4,3,2,1,0:T(8,128)(2,1)S(1)} %get-tuple-element.23.refs_5_.refs_4_.refs_7_), channel_id=1, source_target_pairs={{0,1},{1,2},{2,3},{4,5},{5,6},{6,7}} | collective-permute-start | bytes 3145736 | tf_op jit(solution)/shard_map/ppermute | solution.py:543
  6.6 0.7 copy-start
  7.3 0.7 copy-start.2
  19.3 0.7 copy-start.8
  20.0 15.0 %copy-start.9 = (f32[5,256]{1,0:T(8,128)S(1)}, f32[5,256]{1,0:T(8,128)}, u32[]{:S(2)}) copy-start(f32[5,256]{1,0:T(8,128)} %refs_2_.23) | copy-start | bytes 15364
  33.0 17.7 %copy-start.1 = (f32[4,256]{1,0:T(4,128)S(1)}, f32[4,256]{1,0:T(4,128)}, u32[]{:S(2)}) copy-start(f32[4,256]{1,0:T(4,128)} %refs_2_.21) | copy-start | bytes 12292
  33.0 17.7 %copy-start.3 = (f32[4,256]{1,0:T(4,128)S(1)}, f32[4,256]{1,0:T(4,128)}, u32[]{:S(2)}) copy-start(f32[4,256]{1,0:T(4,128)} %refs_3_.5) | copy-start | bytes 12292
  33.0 24.1 %collective-permute-start.2 = (bf16[1,32,4,16,256]{4,3,2,1,0:T(8,128)(2,1)S(1)}, bf16[1,32,4,16,256]{4,3,2,1,0:T(8,128)(2,1)S(1)}, u32[]{:S(2)}, u32[]{:S(2)}) collective-permute-start(bf16[1,32,4,16,256]{4,3,2,1,0:T(8,128)(2,1)S(1)} %get-tuple-element.27.refs_5_), channel_id=1, source_target_pairs={{0,1},{1,2},{2,3},{4,5},{5,6},{6,7}} | collective-permute-start | bytes 3145736 | tf_op jit(solution)/shard_map/ppermute | solution.py:543
  48.6 21.2 %collective-permute-start.4 = (bf16[1,32,4,16,256]{4,3,2,1,0:T(8,128)(2,1)S(1)}, bf16[1,32,4,16,256]{4,3,2,1,0:T(8,128)(2,1)S(1)}, u32[]{:S(2)}, u32[]{:S(2)}) collective-permute-start(bf16[1,32,4,16,256]{4,3,2,1,0:T(8,128)(2,1)S(1)} %get-tuple-element.28.refs_4_.refs_5_), channel_id=1, source_target_pairs={{0,1},{1,2},{2,3},{4,5},{5,6},{6,7}} | collective-permute-start | bytes 3145736 | tf_op jit(solution)/shard_map/ppermute | solution.py:543
  106.7 204.6 %collective-permute-start.5 = (bf16[2,64,8,16,256]{4,3,2,1,0:T(8,128)(2,1)}, bf16[2,64,8,16,256]{4,3,2,1,0:T(8,128)(2,1)}, u32[]{:S(2)}, u32[]{:S(2)}) collective-permute-start(bf16[2,64,8,16,256]{4,3,2,1,0:T(8,128)(2,1)} %get-tuple-element.33.refs_5_.refs_6_.refs_8_.refs_9_), channel_id=1, source_target_pairs={{0,1},{1,2},{2,3},{4,5},{5,6},{6,7}} | collective-permute-start | bytes 25165832 | tf_op jit(solution)/shard_map/ppermute | solution.py:543
  109.1 103.8 %collective-permute-start.3 = (bf16[1,32,4,16,256]{4,3,2,1,0:T(8,128)(2,1)S(1)}, bf16[1,32,4,16,256]{4,3,2,1,0:T(8,128)(2,1)S(1)}, u32[]{:S(2)}, u32[]{:S(2)}) collective-permute-start(bf16[1,32,4,16,256]{4,3,2,1,0:T(8,128)(2,1)S(1)} %get-tuple-element.29.xb_ref), channel_id=1, source_target_pairs={{0,1},{1,2},{2,3},{4,5},{5,6},{6,7}} | collective-permute-start | bytes 3145736 | tf_op jit(solution)/shard_map/ppermute | solution.py:543
  241.6 0.6 copy-start.6
  309.0 70.8 %copy-start.4 = (f32[2,2,8,256]{3,2,1,0:T(8,128)S(1)}, f32[2,2,8,256]{3,2,1,0:T(8,128)}, u32[]{:S(2)}) copy-start(f32[2,2,8,256]{3,2,1,0:T(8,128)} %get-tuple-element.36.refs_1_) | copy-start | bytes 98308
  309.0 148.0 %collective-permute-start.6 = (bf16[2,64,8,16,256]{4,3,2,1,0:T(8,128)(2,1)}, bf16[2,64,8,16,256]{4,3,2,1,0:T(8,128)(2,1)}, u32[]{:S(2)}, u32[]{:S(2)}) collective-permute-start(bf16[2,64,8,16,256]{4,3,2,1,0:T(8,128)(2,1)} %get-tuple-element.37.refs_5_.refs_6_), channel_id=1, source_target_pairs={{0,1},{1,2},{2,3},{4,5},{5,6},{6,7}} | collective-permute-start | bytes 25165832 | tf_op jit(solution)/shard_map/ppermute | solution.py:543
  379.9 0.8 copy-start.5
  386.6 0.6 copy-start.7
